TPU v7x, 32 devices: a whole 2x2x4 slice. The times are simulated.
32 devices in a mesh: wide: 8 (over y, x, core), narrow: 4 (over z).
Axes of the slice: x: 2, y: 2, z: 4, core: 2. Of those that a mesh axis runs over, the one named last changes fastest.
Arguments:
- inputs: bfloat16 [3152, 1024], P('wide', 'narrow'), may hold values from -6 to 6
- norm_gain: float32 [2, 2, 1024], P(None, None, 'narrow'), may hold values from 0.5 to 1.5
- norm_bias: float32 [2, 2, 1024], P(None, None, 'narrow'), may hold values from -3 to 3
- w_qkv: bfloat16 [2, 1024, 3, 1024], P(None, 'wide', None, 'narrow')
- b_qv: float32 [2, 2, 1024], P(None, None, 'narrow'), may hold values from -3 to 3
- w_out: bfloat16 [2, 1024, 1024], P(None, 'narrow', 'wide'), may hold values from -0.75 to 0.75
- b_out: float32 [2, 1024], P(None, 'narrow'), may hold values from -3 to 3
- w_up: bfloat16 [2, 1024, 4096], P(None, 'wide', 'narrow'), may hold values from -0.1875 to 0.1875
- b_up: float32 [2, 4096], P(None, 'narrow'), may hold values from -3 to 3
- w_down: bfloat16 [2, 4096, 1024], P(None, 'narrow', 'wide'), may hold values from -0.09375 to 0.09375
- b_down: float32 [2, 1024], P(None, 'narrow'), may hold values from -3 to 3
- cotangent: bfloat16 [3152, 1024], P('wide', 'narrow'), may hold values from -6 to 6
Outputs:
- output: float32 [3152, 1024], P('wide', 'narrow')
- grad_input: float32 [3152, 1024], P('wide', 'narrow')
- grad_norm_gain: float32 [2, 2, 1024], P(None, None, 'narrow')
- grad_norm_bias: float32 [2, 2, 1024], P(None, None, 'narrow')
- grad_w_qkv: float32 [2, 1024, 3, 1024], P(None, 'wide', None, 'narrow')
- grad_b_qv: float32 [2, 2, 1024], P(None, None, 'narrow')
- grad_w_out: float32 [2, 1024, 1024], P(None, 'narrow', 'wide')
- grad_b_out: float32 [2, 1024], P(None, 'narrow')
- grad_w_up: float32 [2, 1024, 4096], P(None, 'wide', 'narrow')
- grad_b_up: float32 [2, 4096], P(None, 'narrow')
- grad_w_down: float32 [2, 4096, 1024], P(None, 'narrow', 'wide')
- grad_b_down: float32 [2, 1024], P(None, 'narrow')
All inputs are finite; a program needn't handle non-finite values.
Results may differ from a plain program's by a relative error of at most 0.014.
Values may be sent and summed in bfloat16 or wider, within the bound.
A program may use at most 128 MiB of HBM per device.

v0:
```python
import math

import jax
import jax.numpy as jnp
from jax import lax
from jax.sharding import PartitionSpec as P

D = 1024
HEAD_DIM = 64
SEQ = 197
LAYERS = 2


eps = 1e-06


def gelu_value(pre_act):
    return 0.5 * pre_act * (1.0 + lax.erf(pre_act * 0.7071067811865476))


def gelu_slope(pre_act):
    normal_cdf = 0.5 * (1.0 + lax.erf(pre_act * 0.7071067811865476))
    return normal_cdf + pre_act * jnp.exp(-0.5 * pre_act * pre_act) * 0.3989422804014327


def contract_rows(former, latter):
    return lax.dot_general(
        former, latter, (((0,), (0,)), ((), ())), preferred_element_type=jnp.float32
    )


def times_transpose(former, latter):
    return lax.dot_general(
        former, latter, (((1,), (1,)), ((), ())), preferred_element_type=jnp.float32
    )


def norm_forward(residual, gain_row, shift_row):
    totals, squares = lax.psum(
        (jnp.sum(residual, axis=1), jnp.sum(residual * residual, axis=1)), "narrow"
    )
    center = totals / D
    spread = lax.rsqrt(squares / D - center * center + eps)
    normed = (residual - center[:, None]) * spread[:, None]
    return (normed, spread, (normed * gain_row + shift_row).astype(jnp.bfloat16))


def norm_backward(upstream, normed, spread, gain_row):
    scaled = upstream * gain_row
    first_sum, second_sum = lax.psum(
        (jnp.sum(scaled, axis=1), jnp.sum(scaled * normed, axis=1)), "narrow"
    )
    corrected = scaled - (first_sum / D)[:, None] - normed * (second_sum / D)[:, None]
    return (
        corrected * spread[:, None],
        jnp.sum(upstream * normed, axis=0),
        jnp.sum(upstream, axis=0),
    )


def project_in(normed_act, weight):
    product = jnp.dot(
        lax.all_gather(normed_act, "narrow", axis=1, tiled=True),
        weight,
        preferred_element_type=jnp.float32,
    )
    return (product, normed_act)


def input_weight_grad(normed_act, grad_rounded):
    return contract_rows(lax.all_gather(normed_act, "narrow", axis=1, tiled=True), grad_rounded)


def project_out(local_rounded, weight_cols, bias_row):
    partial_sum = jnp.dot(local_rounded, weight_cols, preferred_element_type=jnp.float32)
    return lax.psum_scatter(partial_sum, "narrow", scatter_dimension=1, tiled=True) + bias_row


def gather_grad(upstream):
    return lax.all_gather(upstream.astype(jnp.bfloat16), "narrow", axis=1, tiled=True)


def sum_input_grad(partial_sum):
    return lax.psum_scatter(partial_sum, "narrow", scatter_dimension=1, tiled=True)


def split_heads(matrix):
    images = matrix.shape[0] // SEQ
    return matrix.reshape(images, SEQ, matrix.shape[1] // HEAD_DIM, HEAD_DIM)


def attention_forward(queries, key_rows, values):
    factor = 1.0 / math.sqrt(HEAD_DIM)
    scores = (
        jnp.einsum(
            "ishd,ithd->ihst",
            split_heads(queries),
            split_heads(key_rows),
            preferred_element_type=jnp.float32,
        )
        * factor
    )
    row_max = jnp.max(scores, axis=-1, keepdims=True)
    logsum = row_max + jnp.log(jnp.sum(jnp.exp(scores - row_max), axis=-1, keepdims=True))
    rounded_p = jnp.exp(scores - logsum).astype(jnp.bfloat16)
    attended = jnp.einsum(
        "ihst,ithd->ishd", rounded_p, split_heads(values), preferred_element_type=jnp.float32
    )
    return (attended.reshape(queries.shape).astype(jnp.bfloat16), logsum)


def attention_backward(queries, key_rows, values, logsum, grad_mixed):
    factor = 1.0 / math.sqrt(HEAD_DIM)
    query_heads = split_heads(queries)
    key_heads = split_heads(key_rows)
    value_heads = split_heads(values)
    grad_heads = split_heads(grad_mixed)
    scores = (
        jnp.einsum("ishd,ithd->ihst", query_heads, key_heads, preferred_element_type=jnp.float32)
        * factor
    )
    probability = jnp.exp(scores - logsum)
    rounded_p = probability.astype(jnp.bfloat16)
    grad_values = jnp.einsum(
        "ihst,ishd->ithd", rounded_p, grad_heads, preferred_element_type=jnp.float32
    )
    grad_probs = jnp.einsum(
        "ishd,ithd->ihst", grad_heads, value_heads, preferred_element_type=jnp.float32
    )
    row_dot = jnp.sum(probability * grad_probs, axis=-1, keepdims=True)
    grad_scores = (probability * (grad_probs - row_dot) * factor).astype(jnp.bfloat16)
    grad_queries = jnp.einsum(
        "ihst,ithd->ishd", grad_scores, key_heads, preferred_element_type=jnp.float32
    )
    grad_keys = jnp.einsum(
        "ihst,ishd->ithd", grad_scores, query_heads, preferred_element_type=jnp.float32
    )
    flat_shape = queries.shape
    return (
        grad_queries.reshape(flat_shape),
        grad_keys.reshape(flat_shape),
        grad_values.reshape(flat_shape),
    )


def body(
    inputs, norm_gain, norm_bias, w_qkv, b_qv, w_out, b_out, w_up, b_up, w_down, b_down, cotangent
):
    local_width = inputs.shape[1]
    residual = inputs.astype(jnp.float32)
    stored = []
    for number in range(LAYERS):
        qkv_rows, out_cols, up_rows, down_cols = (
            lax.all_gather(w_qkv[number], "wide", axis=0, tiled=True),
            lax.all_gather(w_out[number], "wide", axis=1, tiled=True),
            lax.all_gather(w_up[number], "wide", axis=0, tiled=True),
            lax.all_gather(w_down[number], "wide", axis=1, tiled=True),
        )
        qkv_joined = qkv_rows.reshape(D, 3 * local_width)
        normed_one, spread_one, act_one = norm_forward(
            residual, norm_gain[number, 0], norm_bias[number, 0]
        )
        qkv_product, whole_one = project_in(act_one, qkv_joined)
        queries = (qkv_product[:, :local_width] + b_qv[number, 0]).astype(jnp.bfloat16)
        key_rows = qkv_product[:, local_width : 2 * local_width].astype(jnp.bfloat16)
        values = (qkv_product[:, 2 * local_width :] + b_qv[number, 1]).astype(jnp.bfloat16)
        attended, logsum = attention_forward(queries, key_rows, values)
        middle = residual + project_out(attended, out_cols, b_out[number])
        normed_two, spread_two, act_two = norm_forward(
            middle, norm_gain[number, 1], norm_bias[number, 1]
        )
        up_product, whole_two = project_in(act_two, up_rows)
        pre_hidden = up_product + b_up[number]
        hidden = gelu_value(pre_hidden).astype(jnp.bfloat16)
        stored.append(
            (
                qkv_joined,
                out_cols,
                up_rows,
                down_cols,
                normed_one,
                spread_one,
                act_one,
                whole_one,
                queries,
                key_rows,
                values,
                attended,
                logsum,
                normed_two,
                spread_two,
                act_two,
                whole_two,
                pre_hidden,
                hidden,
            )
        )
        residual = middle + project_out(hidden, down_cols, b_down[number])
    upstream = cotangent.astype(jnp.float32)
    weight_grads = [None] * LAYERS
    small_parts = [None] * LAYERS
    for number in reversed(range(LAYERS)):
        (
            qkv_joined,
            out_cols,
            up_rows,
            down_cols,
            normed_one,
            spread_one,
            act_one,
            whole_one,
            queries,
            key_rows,
            values,
            attended,
            logsum,
            normed_two,
            spread_two,
            act_two,
            whole_two,
            pre_hidden,
            hidden,
        ) = stored[number]
        grad_whole = gather_grad(upstream)
        grad_down = contract_rows(hidden, grad_whole)
        grad_pre = times_transpose(grad_whole, down_cols) * gelu_slope(pre_hidden)
        grad_pre_b = grad_pre.astype(jnp.bfloat16)
        grad_up = input_weight_grad(act_two, grad_pre_b)
        grad_act_two = sum_input_grad(times_transpose(grad_pre_b, up_rows))
        grad_norm_two, gain_two, shift_two = norm_backward(
            grad_act_two, normed_two, spread_two, norm_gain[number, 1]
        )
        grad_middle = upstream + grad_norm_two
        middle_whole = gather_grad(grad_middle)
        grad_out_w = contract_rows(attended, middle_whole)
        grad_mixed = times_transpose(middle_whole, out_cols).astype(jnp.bfloat16)
        grad_queries, grad_keys, grad_values = attention_backward(
            queries, key_rows, values, logsum, grad_mixed
        )
        grad_qkv_b = jnp.concatenate([grad_queries, grad_keys, grad_values], axis=1).astype(
            jnp.bfloat16
        )
        grad_qkv_w = input_weight_grad(act_one, grad_qkv_b).reshape(D, 3, local_width)
        grad_act_one = sum_input_grad(times_transpose(grad_qkv_b, qkv_joined))
        grad_norm_one, gain_one, shift_one = norm_backward(
            grad_act_one, normed_one, spread_one, norm_gain[number, 0]
        )
        small_parts[number] = (
            jnp.stack([gain_one, gain_two]),
            jnp.stack([shift_one, shift_two]),
            jnp.stack([jnp.sum(grad_queries, axis=0), jnp.sum(grad_values, axis=0)]),
            jnp.sum(grad_middle, axis=0),
            jnp.sum(grad_pre, axis=0),
            jnp.sum(upstream, axis=0),
        )
        weight_grads[number] = (grad_qkv_w, grad_out_w, grad_up, grad_down)
        upstream = grad_middle + grad_norm_one
    stacked = (
        lax.psum_scatter(
            jnp.stack([entry_grads[0] for entry_grads in weight_grads]).astype(jnp.bfloat16),
            "wide",
            scatter_dimension=1,
            tiled=True,
        ).astype(jnp.float32),
        lax.psum_scatter(
            jnp.stack([entry_grads[1] for entry_grads in weight_grads]).astype(jnp.bfloat16),
            "wide",
            scatter_dimension=2,
            tiled=True,
        ).astype(jnp.float32),
        lax.psum_scatter(
            jnp.stack([entry_grads[2] for entry_grads in weight_grads]).astype(jnp.bfloat16),
            "wide",
            scatter_dimension=1,
            tiled=True,
        ).astype(jnp.float32),
        lax.psum_scatter(
            jnp.stack([entry_grads[3] for entry_grads in weight_grads]).astype(jnp.bfloat16),
            "wide",
            scatter_dimension=2,
            tiled=True,
        ).astype(jnp.float32),
    )
    small_sums = lax.psum(
        (
            jnp.stack([entry_parts[0] for entry_parts in small_parts]),
            jnp.stack([entry_parts[1] for entry_parts in small_parts]),
            jnp.stack([entry_parts[2] for entry_parts in small_parts]),
            jnp.stack([entry_parts[3] for entry_parts in small_parts]),
            jnp.stack([entry_parts[4] for entry_parts in small_parts]),
            jnp.stack([entry_parts[5] for entry_parts in small_parts]),
        ),
        "wide",
    )
    return (
        residual,
        upstream,
        small_sums[0],
        small_sums[1],
        stacked[0],
        small_sums[2],
        stacked[1],
        small_sums[3],
        stacked[2],
        small_sums[4],
        stacked[3],
        small_sums[5],
    )


def solution(mesh):
    placed = (
        P("wide", "narrow"),
        P(None, None, "narrow"),
        P(None, None, "narrow"),
        P(None, "wide", None, "narrow"),
        P(None, None, "narrow"),
        P(None, "narrow", "wide"),
        P(None, "narrow"),
        P(None, "wide", "narrow"),
        P(None, "narrow"),
        P(None, "narrow", "wide"),
        P(None, "narrow"),
        P("wide", "narrow"),
    )
    return jax.shard_map(
        body,
        mesh=mesh,
        in_specs=placed,
        out_specs=(
            P("wide", "narrow"),
            P("wide", "narrow"),
            P(None, None, "narrow"),
            P(None, None, "narrow"),
            P(None, "wide", None, "narrow"),
            P(None, None, "narrow"),
            P(None, "narrow", "wide"),
            P(None, "narrow"),
            P(None, "wide", "narrow"),
            P(None, "narrow"),
            P(None, "narrow", "wide"),
            P(None, "narrow"),
        ),
        check_vma=False,
    )
```

profile of v0, /device:TPU:0, one launch (start us, length us, event | category | flops | bytes accessed | tf_op | source)
XLA Modules:
  0.0 864.2 jit_solution(8709687083352596518)
XLA Ops:
  11.1 13.5 %all-reduce.8 = (f32[394]{0:T(512)S(1)}, f32[394]{0:T(512)S(1)}) all-reduce(f32[394]{0:T(512)S(1)} %get-tuple-element.35, f32[394]{0:T(512)S(1)} %get-tuple-element.34), channel_id=1, replica_groups=mesh['wide'=8,'narrow'=4] {'narrow'}, use_global_device_ids=true, to_apply=%region_3.0 | all-reduce | flops 788 | bytes 6304 | tf_op jit(solution)/shard_map/psum | solution.py:39
  24.6 10.6 %all-gather.1 = bf16[1,256,1024]{2,1,0:T(8,128)(2,1)S(1)} all-gather(bf16[1,256,128]{2,1,0:T(8,128)(2,1)S(1)} %get-tuple-element.88), channel_id=3, replica_groups=mesh['wide'=8,'narrow'=4] {'wide'}, dimensions={2}, use_global_device_ids=true | all-gather | bytes 589824 | tf_op jit(solution)/shard_map/all_gather | solution.py:155
  37.8 18.3 %all_gather.52 = bf16[394,1024]{1,0:T(8,128)(2,1)S(1)} all-gather(bf16[394,256]{1,0:T(8,128)(2,1)S(1)} %fusion.104), channel_id=1, replica_groups=mesh['wide'=8,'narrow'=4] {'narrow'}, dimensions={1}, use_global_device_ids=true | all-gather | bytes 1008640 | tf_op jit(solution)/shard_map/all_gather | solution.py:63
  68.3 32.7 %reduce-scatter.17.cloned.1.call-done = f32[394,256]{1,0:T(8,128)} async-done(((f32[394,1024]{1,0:T(8,128)}), f32[394,256]{1,0:T(8,128)}) %reduce-scatter.17.cloned.1.call-update) | async-done | bytes 403472 | tf_op jit(solution)/shard_map/reduce_scatter | solution.py:76
  102.2 9.7 %all-reduce.7 = (f32[394]{0:T(512)S(1)}, f32[394]{0:T(512)S(1)}) all-reduce(f32[394]{0:T(512)S(1)} %get-tuple-element.33, f32[394]{0:T(512)S(1)} %get-tuple-element.32), channel_id=1, replica_groups=mesh['wide'=8,'narrow'=4] {'narrow'}, use_global_device_ids=true, to_apply=%region_10.0 | all-reduce | flops 788 | bytes 6304 | tf_op jit(solution)/shard_map/psum | solution.py:39
  112.1 17.3 %all_gather.55 = bf16[394,1024]{1,0:T(8,128)(2,1)S(1)} all-gather(bf16[394,256]{1,0:T(8,128)(2,1)S(1)} %add_convert_fusion.2), channel_id=1, replica_groups=mesh['wide'=8,'narrow'=4] {'narrow'}, dimensions={1}, use_global_device_ids=true | all-gather | bytes 1008640 | tf_op jit(solution)/shard_map/all_gather | solution.py:63
  130.2 4.3 multiply_convert_fusion.3
  134.5 26.2 %all-gather.19.cloned.1.call-done = bf16[1,1024,1024]{2,1,0:T(8,128)(2,1)} async-done(((bf16[1,1024,128]{2,1,0:T(8,128)(2,1)}), bf16[1,1024,1024]{2,1,0:T(8,128)(2,1)}) %all-gather.19.cloned.1.call-update) | async-done | bytes 2097168 | tf_op jit(solution)/shard_map/all_gather | solution.py:157
  160.6 4.0 fusion.12
  166.5 10.9 %all-gather.5 = bf16[1,256,1024]{2,1,0:T(8,128)(2,1)} all-gather(bf16[1,256,128]{2,1,0:T(8,128)(2,1)S(1)} %get-tuple-element.87), channel_id=7, replica_groups=mesh['wide'=8,'narrow'=4] {'wide'}, dimensions={2}, use_global_device_ids=true | all-gather | bytes 589824 | tf_op jit(solution)/shard_map/all_gather | solution.py:155
  177.4 23.9 %reduce-scatter.19.cloned.1.call-done = f32[394,256]{1,0:T(8,128)} async-done(((f32[394,1024]{1,0:T(8,128)}), f32[394,256]{1,0:T(8,128)}) %reduce-scatter.19.cloned.1.call-update) | async-done | bytes 403472 | tf_op jit(solution)/shard_map/reduce_scatter | solution.py:76
  202.5 9.7 %all-reduce.6 = (f32[394]{0:T(512)S(1)}, f32[394]{0:T(512)S(1)}) all-reduce(f32[394]{0:T(512)S(1)} %get-tuple-element.31, f32[394]{0:T(512)S(1)} %get-tuple-element.30), channel_id=1, replica_groups=mesh['wide'=8,'narrow'=4] {'narrow'}, use_global_device_ids=true, to_apply=%region_15.0 | all-reduce | flops 788 | bytes 6304 | tf_op jit(solution)/shard_map/psum | solution.py:39
  212.4 17.5 %all_gather.58 = bf16[394,1024]{1,0:T(8,128)(2,1)S(1)} all-gather(bf16[394,256]{1,0:T(8,128)(2,1)S(1)} %add_convert_fusion.1), channel_id=1, replica_groups=mesh['wide'=8,'narrow'=4] {'narrow'}, dimensions={1}, use_global_device_ids=true | all-gather | bytes 1008640 | tf_op jit(solution)/shard_map/all_gather | solution.py:63
  241.8 2.7 fusion.93
  246.1 28.5 %all_gather.64 = bf16[394,1024]{1,0:T(8,128)(2,1)} all-gather(bf16[394,256]{1,0:T(8,128)(2,1)} %param.23), channel_id=1, replica_groups=mesh['wide'=8,'narrow'=4] {'narrow'}, dimensions={1}, use_global_device_ids=true | all-gather | bytes 1008640 | tf_op jit(solution)/shard_map/all_gather | solution.py:80
  274.6 15.7 %reduce-scatter.21.cloned.1.call-done = f32[394,256]{1,0:T(8,128)} async-done(((f32[394,1024]{1,0:T(8,128)}), f32[394,256]{1,0:T(8,128)}) %reduce-scatter.21.cloned.1.call-update) | async-done | bytes 403472 | tf_op jit(solution)/shard_map/reduce_scatter | solution.py:76
  292.2 11.3 %all-reduce.5 = (f32[394]{0:T(512)S(1)}, f32[394]{0:T(512)S(1)}) all-reduce(f32[394]{0:T(512)S(1)} %get-tuple-element.29, f32[394]{0:T(512)S(1)} %get-tuple-element.28), channel_id=1, replica_groups=mesh['wide'=8,'narrow'=4] {'narrow'}, use_global_device_ids=true, to_apply=%region_22.0 | all-reduce | flops 788 | bytes 6304 | tf_op jit(solution)/shard_map/psum | solution.py:39
  304.7 17.9 %all_gather.61 = bf16[394,1024]{1,0:T(8,128)(2,1)} all-gather(bf16[394,256]{1,0:T(8,128)(2,1)S(1)} %add_convert_fusion), channel_id=1, replica_groups=mesh['wide'=8,'narrow'=4] {'narrow'}, dimensions={1}, use_global_device_ids=true | all-gather | bytes 1008640 | tf_op jit(solution)/shard_map/all_gather | solution.py:63
  322.6 4.4 multiply_convert_fusion.2
  327.1 24.1 %all-gather.25.cloned.1.call-done = bf16[1,1024,1024]{2,1,0:T(8,128)(2,1)} async-done(((bf16[1,1024,128]{2,1,0:T(8,128)(2,1)}), bf16[1,1024,1024]{2,1,0:T(8,128)(2,1)}) %all-gather.25.cloned.1.call-update) | async-done | bytes 2097168 | tf_op jit(solution)/shard_map/all_gather | solution.py:157
  351.1 4.5 fusion.157
  358.9 4.0 fusion.4
  363.0 32.4 %reduce-scatter.25.cloned.1.call-done = f32[394,256]{1,0:T(8,128)} async-done(((f32[394,1024]{1,0:T(8,128)}), f32[394,256]{1,0:T(8,128)}) %reduce-scatter.25.cloned.1.call-update) | async-done | bytes 403472 | tf_op jit(solution)/shard_map/reduce_scatter | solution.py:84
  396.9 9.8 %all-reduce.4 = (f32[394]{0:T(512)S(1)}, f32[394]{0:T(512)S(1)}) all-reduce(f32[394]{0:T(512)S(1)} %get-tuple-element.17, f32[394]{0:T(512)S(1)} %get-tuple-element.21), channel_id=1, replica_groups=mesh['wide'=8,'narrow'=4] {'narrow'}, use_global_device_ids=true, to_apply=%region_28.0 | all-reduce | flops 788 | bytes 6304 | tf_op jit(solution)/shard_map/psum | solution.py:50
  406.7 26.4 %reduce-scatter.23.cloned.1.call-done = f32[394,256]{1,0:T(8,128)} async-done(((f32[394,1024]{1,0:T(8,128)}), f32[394,256]{1,0:T(8,128)}) %reduce-scatter.23.cloned.1.call-update) | async-done | bytes 403472 | tf_op jit(solution)/shard_map/reduce_scatter | solution.py:76
  436.2 18.5 %all_gather.65 = bf16[394,1024]{1,0:T(8,128)(2,1)S(1)} all-gather(bf16[394,256]{1,0:T(8,128)(2,1)S(1)} %convert_element_type.131), channel_id=1, replica_groups=mesh['wide'=8,'narrow'=4] {'narrow'}, dimensions={1}, use_global_device_ids=true | all-gather | bytes 1008640 | tf_op jit(solution)/shard_map/all_gather | solution.py:80
  464.3 3.5 fusion.72
  467.8 4.1 fusion.139
  476.1 3.4 fusion.162
  479.6 36.2 %reduce-scatter.27.cloned.1.call-done = f32[394,256]{1,0:T(8,128)} async-done(((f32[394,1024]{1,0:T(8,128)}), f32[394,256]{1,0:T(8,128)}) %reduce-scatter.27.cloned.1.call-update) | async-done | bytes 403472 | tf_op jit(solution)/shard_map/reduce_scatter | solution.py:84
  517.1 9.7 %all-reduce.3 = (f32[394]{0:T(512)S(1)}, f32[394]{0:T(512)S(1)}) all-reduce(f32[394]{0:T(512)S(1)} %get-tuple-element.15, f32[394]{0:T(512)S(1)} %get-tuple-element.22), channel_id=1, replica_groups=mesh['wide'=8,'narrow'=4] {'narrow'}, use_global_device_ids=true, to_apply=%region_34.0 | all-reduce | flops 788 | bytes 6304 | tf_op jit(solution)/shard_map/psum | solution.py:50
  528.3 17.3 %all_gather.66 = bf16[394,1024]{1,0:T(8,128)(2,1)S(1)} all-gather(bf16[394,256]{1,0:T(8,128)(2,1)S(1)} %convert_element_type.134), channel_id=1, replica_groups=mesh['wide'=8,'narrow'=4] {'narrow'}, dimensions={1}, use_global_device_ids=true | all-gather | bytes 1008640 | tf_op jit(solution)/shard_map/all_gather | solution.py:80
  545.6 3.8 fusion.158
  556.0 32.4 %reduce-scatter.29.cloned.1.call-done = f32[394,256]{1,0:T(8,128)} async-done(((f32[394,1024]{1,0:T(8,128)}), f32[394,256]{1,0:T(8,128)}) %reduce-scatter.29.cloned.1.call-update) | async-done | bytes 403472 | tf_op jit(solution)/shard_map/reduce_scatter | solution.py:84
  589.8 9.7 %all-reduce.2 = (f32[394]{0:T(512)S(1)}, f32[394]{0:T(512)S(1)}) all-reduce(f32[394]{0:T(512)S(1)} %get-tuple-element.13, f32[394]{0:T(512)S(1)} %get-tuple-element.23), channel_id=1, replica_groups=mesh['wide'=8,'narrow'=4] {'narrow'}, use_global_device_ids=true, to_apply=%region_39.0 | all-reduce | flops 788 | bytes 6304 | tf_op jit(solution)/shard_map/psum | solution.py:50
  600.9 17.4 %all_gather.67 = bf16[394,1024]{1,0:T(8,128)(2,1)S(1)} all-gather(bf16[394,256]{1,0:T(8,128)(2,1)S(1)} %convert_element_type.136), channel_id=1, replica_groups=mesh['wide'=8,'narrow'=4] {'narrow'}, dimensions={1}, use_global_device_ids=true | all-gather | bytes 1008640 | tf_op jit(solution)/shard_map/all_gather | solution.py:80
  630.8 11.4 %copy.148 = bf16[2,1024,1024]{1,0,2:T(2,128)(2,1)} copy(bf16[2,1024,1024]{2,1,0:T(8,128)(2,1)} %pad_maximum_fusion.1) | data formatting | bytes 8388608
  642.2 5.8 copy.169
  660.2 2.7 fusion.75
  663.4 2.8 fusion.137
  667.6 3.5 fusion.164
  674.3 3.7 convolution_convert_fusion.1
  684.5 29.4 %reduce-scatter.39.cloned.1.call-done = bf16[128,2048]{1,0:T(8,128)(2,1)} async-done(((bf16[1024,2048]{1,0:T(8,128)(2,1)}), bf16[128,2048]{1,0:T(8,128)(2,1)}) %reduce-scatter.39.cloned.1.call-update) | async-done | bytes 524304
  716.9 51.3 %reduce-scatter.35.cloned.1.call-done = bf16[2,128,1024]{2,1,0:T(8,128)(2,1)} async-done(((bf16[2,1024,1024]{2,1,0:T(8,128)(2,1)}), bf16[2,128,1024]{2,1,0:T(8,128)(2,1)}) %reduce-scatter.35.cloned.1.call-update) | async-done | bytes 524304 | tf_op jit(solution)/shard_map/reduce_scatter | solution.py:271
  770.3 36.5 %reduce-scatter.31.cloned.1.call-done = f32[394,256]{1,0:T(8,128)} async-done(((f32[394,1024]{1,0:T(8,128)}), f32[394,256]{1,0:T(8,128)}) %reduce-scatter.31.cloned.1.call-update) | async-done | bytes 403472 | tf_op jit(solution)/shard_map/reduce_scatter | solution.py:84
  808.2 9.7 %all-reduce.1 = (f32[394]{0:T(512)S(1)}, f32[394]{0:T(512)S(1)}) all-reduce(f32[394]{0:T(512)S(1)} %get-tuple-element.19, f32[394]{0:T(512)S(1)} %get-tuple-element.20), channel_id=1, replica_groups=mesh['wide'=8,'narrow'=4] {'narrow'}, use_global_device_ids=true, to_apply=%region_45.0 | all-reduce | flops 788 | bytes 6304 | tf_op jit(solution)/shard_map/psum | solution.py:50
  817.9 23.7 %all-reduce = (f32[2,2,256]{2,1,0:T(2,128)}, f32[2,2,256]{2,1,0:T(2,128)}, f32[2,2,256]{2,1,0:T(2,128)}, f32[2,256]{1,0:T(2,128)}, f32[2,1024]{1,0:T(2,128)}, /*index=5*/f32[2,256]{1,0:T(2,128)}) all-reduce(f32[2,2,256]{2,1,0:T(2,128)S(1)} %pad_maximum_fusion.5, ...), channel_id=1, replica_groups=mesh['wide'=8,'narrow'=4] {'wide'}, use_global_device_ids=true, to_apply=%region_50.0 | all-reduce | flops 6144 | bytes 49152 | tf_op jit(solution)/shard_map/psum | solution.py:284
  843.7 11.5 %reduce-scatter.33.cloned.1.call-done = bf16[2,128,3,256]{3,1,2,0:T(8,128)(2,1)} async-done(((bf16[2,1024,3,256]{3,1,2,0:T(8,128)(2,1)}), bf16[2,128,3,256]{3,1,2,0:T(8,128)(2,1)}) %reduce-scatter.33.cloned.1.call-update) | async-done | bytes 393232 | tf_op jit(solution)/shard_map/reduce_scatter | solution.py:259
  (343 shorter events, 120.4 us)
Async XLA Ops:
  7.2 30.4 %copy-start.4 = (bf16[394,256]{1,0:T(8,128)(2,1)S(1)}, bf16[394,256]{1,0:T(8,128)(2,1)}, u32[]{:S(2)}) copy-start(bf16[394,256]{1,0:T(8,128)(2,1)} %param.12) | copy-start | bytes 605188
  7.2 28.1 %copy-start.63 = (f32[2,2,256]{2,1,0:T(2,128)S(1)}, f32[2,2,256]{2,1,0:T(2,128)}, u32[]{:S(2)}) copy-start(f32[2,2,256]{2,1,0:T(2,128)} %param.13) | copy-start | bytes 12292
  7.2 28.7 %copy-start.64 = (f32[2,2,256]{2,1,0:T(2,128)S(1)}, f32[2,2,256]{2,1,0:T(2,128)}, u32[]{:S(2)}) copy-start(f32[2,2,256]{2,1,0:T(2,128)} %param.14) | copy-start | bytes 12292
  7.2 29.2 %copy-start.65 = (f32[2,2,256]{2,1,0:T(2,128)S(1)}, f32[2,2,256]{2,1,0:T(2,128)}, u32[]{:S(2)}) copy-start(f32[2,2,256]{2,1,0:T(2,128)} %param.16) | copy-start | bytes 12292
  7.2 48.9 %all-gather.15.cloned.1.call-start = ((), (), s32[]{:S(2)}) async-start(), calls=%async_computation.22 | async-start | bytes 1769472 | tf_op jit(solution)/shard_map/all_gather | solution.py:154
  9.9 91.1 %reduce-scatter.17.cloned.1.call-start = ((), (), s32[]{:S(2)}) async-start(), calls=%async_computation.12 | async-start | bytes 2048000 | tf_op jit(solution)/shard_map/reduce_scatter | solution.py:76
  35.3 28.3 %copy-start.20 = (bf16[1,256,1024]{2,1,0:T(8,128)(2,1)}, bf16[1,256,1024]{2,1,0:T(8,128)(2,1)S(1)}, u32[]{:S(2)}) copy-start(bf16[1,256,1024]{2,1,0:T(8,128)(2,1)S(1)} %all-gather.1) | copy-start | bytes 1572868
  35.9 76.1 %copy-start.54 = (f32[1,1,256]{2,1,0:T(1,128)}, f32[1,1,256]{2,1,0:T(1,128)S(1)}, u32[]{:S(2)}) copy-start(f32[1,1,256]{2,1,0:T(1,128)S(1)} %get-tuple-element.92) | copy-start | bytes 3076
  35.9 176.3 %copy-start.56 = (f32[1,1,256]{2,1,0:T(1,128)}, f32[1,1,256]{2,1,0:T(1,128)S(1)}, u32[]{:S(2)}) copy-start(f32[1,1,256]{2,1,0:T(1,128)S(1)} %get-tuple-element.94) | copy-start | bytes 3076
  65.2 64.9 %all-gather.17.cloned.1.call-start = ((), (), s32[]{:S(2)}) async-start(), calls=%async_computation.23 | async-start | bytes 2359296 | tf_op jit(solution)/shard_map/all_gather | solution.py:156
  66.1 94.5 %all-gather.19.cloned.1.call-start = ((), (), s32[]{:S(2)}) async-start(), calls=%async_computation.24 | async-start | bytes 2359296 | tf_op jit(solution)/shard_map/all_gather | solution.py:157
  67.1 134.2 %reduce-scatter.19.cloned.1.call-start = ((), (), s32[]{:S(2)}) async-start(), calls=%async_computation.13 | async-start | bytes 2048000 | tf_op jit(solution)/shard_map/reduce_scatter | solution.py:76
  102.2 99.1 %copy-start = (f32[394,256]{1,0:T(8,128)}, f32[394,256]{1,0:T(8,128)S(1)}, u32[]{:S(2)}) copy-start(f32[394,256]{1,0:T(8,128)S(1)} %get-tuple-element.66) | copy-start | bytes 1210372
  111.9 22.5 %copy-start.48 = (f32[394]{0:T(512)}, f32[394]{0:T(512)S(1)}, u32[]{:S(2)}) copy-start(f32[394]{0:T(512)S(1)} %get-tuple-element.111) | copy-start | bytes 4732
  111.9 22.5 %copy-start.50 = (f32[394]{0:T(512)}, f32[394]{0:T(512)S(1)}, u32[]{:S(2)}) copy-start(f32[394]{0:T(512)S(1)} %get-tuple-element.112) | copy-start | bytes 4732
  164.7 65.2 %all-gather.21.cloned.1.call-start = ((), (), s32[]{:S(2)}) async-start(), calls=%async_computation.25 | async-start | bytes 1769472 | tf_op jit(solution)/shard_map/all_gather | solution.py:154
  166.4 123.9 %reduce-scatter.21.cloned.1.call-start = ((), (), s32[]{:S(2)}) async-start(), calls=%async_computation.14 | async-start | bytes 2048000 | tf_op jit(solution)/shard_map/reduce_scatter | solution.py:76
  202.5 30.6 %copy-start.2 = (f32[394,256]{1,0:T(8,128)}, f32[394,256]{1,0:T(8,128)S(1)}, u32[]{:S(2)}) copy-start(f32[394,256]{1,0:T(8,128)S(1)} %get-tuple-element.65) | copy-start | bytes 1210372
  244.5 45.8 %copy-start.69 = (f32[1,256]{1,0:T(1,128)S(1)}, f32[1,256]{1,0:T(1,128)}, u32[]{:S(2)}) copy-start(f32[1,256]{1,0:T(1,128)} %get-tuple-element.107) | copy-start | bytes 3076
  244.5 59.0 %copy-start.58 = (f32[1,1,256]{2,1,0:T(1,128)S(1)}, f32[1,1,256]{2,1,0:T(1,128)}, u32[]{:S(2)}) copy-start(f32[1,1,256]{2,1,0:T(1,128)} %get-tuple-element.91) | copy-start | bytes 3076
  244.5 59.0 %copy-start.60 = (f32[1,1,256]{2,1,0:T(1,128)S(1)}, f32[1,1,256]{2,1,0:T(1,128)}, u32[]{:S(2)}) copy-start(f32[1,1,256]{2,1,0:T(1,128)} %get-tuple-element.95) | copy-start | bytes 3076
  244.6 78.0 %all-gather.23.cloned.1.call-start = ((), (), s32[]{:S(2)}) async-start(), calls=%async_computation.26 | async-start | bytes 2359296 | tf_op jit(solution)/shard_map/all_gather | solution.py:156
  245.3 105.8 %all-gather.25.cloned.1.call-start = ((), (), s32[]{:S(2)}) async-start(), calls=%async_computation.27 | async-start | bytes 2359296 | tf_op jit(solution)/shard_map/all_gather | solution.py:157
  246.0 149.4 %reduce-scatter.25.cloned.1.call-start = ((), (), s32[]{:S(2)}) async-start(), calls=%async_computation.16 | async-start | bytes 2048000 | tf_op jit(solution)/shard_map/reduce_scatter | solution.py:84
  274.6 48.0 %copy-start.68 = (f32[1,1024]{1,0:T(1,128)S(1)}, f32[1,1024]{1,0:T(1,128)}, u32[]{:S(2)}) copy-start(f32[1,1024]{1,0:T(1,128)} %get-tuple-element.89) | copy-start | bytes 12292
  358.8 74.3 %reduce-scatter.23.cloned.1.call-start = ((), (), s32[]{:S(2)}) async-start(), calls=%async_computation.15 | async-start | bytes 2048000 | tf_op jit(solution)/shard_map/reduce_scatter | solution.py:76
  362.9 152.9 %reduce-scatter.27.cloned.1.call-start = ((), (), s32[]{:S(2)}) async-start(), calls=%async_computation.17 | async-start | bytes 2048000 | tf_op jit(solution)/shard_map/reduce_scatter | solution.py:84
  433.1 22.5 %copy-start.22 = (bf16[1,256,1024]{2,1,0:T(8,128)(2,1)S(1)}, bf16[1,256,1024]{2,1,0:T(8,128)(2,1)}, u32[]{:S(2)}) copy-start(bf16[1,256,1024]{2,1,0:T(8,128)(2,1)} %all-gather.5) | copy-start | bytes 1572868
  479.5 36.2 %copy-start.3 = (f32[394,256]{1,0:T(8,128)S(1)}, f32[394,256]{1,0:T(8,128)}, u32[]{:S(2)}) copy-start(f32[394,256]{1,0:T(8,128)} %copy-done.2) | copy-start | bytes 1210372
  479.5 36.2 %copy-start.57 = (f32[1,1,256]{2,1,0:T(1,128)S(1)}, f32[1,1,256]{2,1,0:T(1,128)}, u32[]{:S(2)}) copy-start(f32[1,1,256]{2,1,0:T(1,128)} %copy-done.56) | copy-start | bytes 3076
  479.6 47.3 %copy-start.8 = (f32[394,256]{1,0:T(8,128)S(1)}, f32[394,256]{1,0:T(8,128)}, u32[]{:S(2)}) copy-start(f32[394,256]{1,0:T(8,128)} %copy-done.7) | copy-start | bytes 1210372
  479.6 108.8 %reduce-scatter.29.cloned.1.call-start = ((), (), s32[]{:S(2)}) async-start(), calls=%async_computation.18 | async-start | bytes 2048000 | tf_op jit(solution)/shard_map/reduce_scatter | solution.py:84
  526.9 18.8 %copy-start.74 = (bf16[1,1024,1024]{2,1,0:T(8,128)(2,1)S(1)}, bf16[1,1024,1024]{2,1,0:T(8,128)(2,1)}, u32[]{:S(2)}) copy-start(bf16[1,1024,1024]{2,1,0:T(8,128)(2,1)} %all-gather.19.cloned.1.call-done) | copy-start | bytes 6291460
  552.7 35.7 %copy-start.1 = (f32[394,256]{1,0:T(8,128)S(1)}, f32[394,256]{1,0:T(8,128)}, u32[]{:S(2)}) copy-start(f32[394,256]{1,0:T(8,128)} %copy-done) | copy-start | bytes 1210372
  552.7 35.7 %copy-start.49 = (f32[394]{0:T(512)S(1)}, f32[394]{0:T(512)}, u32[]{:S(2)}) copy-start(f32[394]{0:T(512)} %copy-done.48) | copy-start | bytes 4732
  552.7 35.7 %copy-start.51 = (f32[394]{0:T(512)S(1)}, f32[394]{0:T(512)}, u32[]{:S(2)}) copy-start(f32[394]{0:T(512)} %copy-done.50) | copy-start | bytes 4732
  552.7 35.7 %copy-start.55 = (f32[1,1,256]{2,1,0:T(1,128)S(1)}, f32[1,1,256]{2,1,0:T(1,128)}, u32[]{:S(2)}) copy-start(f32[1,1,256]{2,1,0:T(1,128)} %copy-done.54) | copy-start | bytes 3076
  552.7 129.9 %reduce-scatter.37.cloned.1.call-start = ((), (), s32[]{:S(2)}) async-start(), calls=%async_computation.28 | async-start | bytes 1179648
  599.5 19.8 %copy-start.13 = (bf16[394,256]{0,1:T(8,128)(2,1)S(1)}, bf16[394,256]{0,1:T(8,128)(2,1)}, u32[]{:S(2)}) copy-start(bf16[394,256]{0,1:T(8,128)(2,1)} %copy-done.12) | copy-start | bytes 605188
  600.8 18.8 %copy-start.23 = (bf16[1,256,1024]{2,1,0:T(8,128)(2,1)S(1)}, bf16[1,256,1024]{2,1,0:T(8,128)(2,1)}, u32[]{:S(2)}) copy-start(bf16[1,256,1024]{2,1,0:T(8,128)(2,1)} %fusion.63) | copy-start | bytes 1572868
  624.3 89.5 %reduce-scatter.39.cloned.1.call-start = ((), (), s32[]{:S(2)}) async-start(), calls=%async_computation.29 | async-start | bytes 4718592
  648.0 120.1 %reduce-scatter.35.cloned.1.call-start = ((), (), s32[]{:S(2)}) async-start(), calls=%async_computation.21 | async-start | bytes 4718592 | tf_op jit(solution)/shard_map/reduce_scatter | solution.py:271
  655.5 151.3 %reduce-scatter.31.cloned.1.call-start = ((), (), s32[]{:S(2)}) async-start(), calls=%async_computation.19 | async-start | bytes 2048000 | tf_op jit(solution)/shard_map/reduce_scatter | solution.py:84
  671.1 184.1 %reduce-scatter.33.cloned.1.call-start = ((), (), s32[]{:S(2)}) async-start(), calls=%async_computation.20 | async-start | bytes 3538944 | tf_op jit(solution)/shard_map/reduce_scatter | solution.py:259
  715.8 91.0 %copy-start.45 = (f32[394]{0:T(512)S(1)}, f32[394]{0:T(512)}, u32[]{:S(2)}) copy-start(f32[394]{0:T(512)} %copy-done.44) | copy-start | bytes 4732
  715.8 91.0 %copy-start.47 = (f32[394]{0:T(512)S(1)}, f32[394]{0:T(512)}, u32[]{:S(2)}) copy-start(f32[394]{0:T(512)} %copy-done.46) | copy-start | bytes 4732
  715.8 91.0 %copy-start.53 = (f32[1,1,256]{2,1,0:T(1,128)S(1)}, f32[1,1,256]{2,1,0:T(1,128)}, u32[]{:S(2)}) copy-start(f32[1,1,256]{2,1,0:T(1,128)} %copy-done.52) | copy-start | bytes 3076
  715.8 125.8 %copy-start.6 = (f32[394,256]{1,0:T(8,128)S(1)}, f32[394,256]{1,0:T(8,128)}, u32[]{:S(2)}) copy-start(f32[394,256]{1,0:T(8,128)} %copy-done.5) | copy-start | bytes 1210372
  (50 other events, 135.6 us)
Sparse Core Ops, SparseCore 0:
  10.5 29.1 all-gather.14
  65.3 35.6 reduce-scatter.16
  103.5 26.6 all-gather.16
  132.5 28.0 all-gather.18
  164.8 36.4 reduce-scatter.18
  203.6 24.6 all-gather.20
  244.7 45.5 reduce-scatter.20
  292.8 27.7 all-gather.22
  323.0 28.0 all-gather.24
  358.9 36.4 reduce-scatter.24
  397.7 35.3 reduce-scatter.22
  479.7 36.0 reduce-scatter.26
  552.9 35.4 reduce-scatter.28
  624.4 34.9 reduce-scatter.36
  662.6 51.1 reduce-scatter.38
  717.1 51.0 reduce-scatter.34
  770.3 36.4 reduce-scatter.30
  810.0 45.0 reduce-scatter.32
where the time goes:
time: 873 us; the launch traced here: 864 us
  waiting for transfers between devices  381 us (44%)
  blocking collectives  281 us (32%)
  matrix products  84.9 us (10%)
  local copies, waits for them, and re-layouts  67 us (8%)
  other arithmetic  33.6 us (4%)
  between operations  15.6 us (2%)
    reduce_scatter x4, waiting for transfers between devices, sum_input_grad(): lax.psum_scatter(partial_sum, 'narrow', scatter_dimension=1, tiled=True)  137 us
    reduce_scatter x4, waiting for transfers between devices, project_out(): lax.psum_scatter(partial_sum, 'narrow', scatter_dimension=1, tiled=True)  98.7 us
    all_gather x4, blocking collectives, gather_grad(): lax.all_gather(upstream.astype(jnp.bfloat16), 'narrow', axis=1, tiled=True)  81.7 us
    all_gather x4, blocking collectives, project_in(): lax.all_gather(normed_act, 'narrow', axis=1, tiled=True)  71 us
    reduce_scatter x1, waiting for transfers between devices, body(): lax.psum_scatter(jnp.stack([entry_grads[2] for entry_grads in weight_grad...  51.3 us
    all_gather x2, waiting for transfers between devices, body(): lax.all_gather(w_down[number], 'wide', axis=1, tiled=True)  50.2 us
    psum x4, blocking collectives, norm_forward(): lax.psum((jnp.sum(residual, axis=1), jnp.sum(residual * residual, axis=1)...  44.1 us
    unnamed x174, local copies, waits for them, and re-layouts  40.1 us
  transfers between devices with their start and end apart: 18, of which 14 were waited for; matrix products, arithmetic and copies ran while one was open for 11% of the time, Pallas kernels for 0%

commit v1 on v0

v1 whole, which is shorter than its diff:
```python
import functools
import math

import jax
import jax.numpy as jnp
from jax import lax
from jax.experimental import pallas as pl
from jax.experimental.pallas import tpu as pltpu
from jax.sharding import PartitionSpec as P

D = 1024
HEAD_DIM = 64
SEQ = 197
LAYERS = 2
EPS = 1e-06
ROWS = 208
KEYS = 256
MESH = pl.DeviceIdType.MESH
F32 = jnp.float32
BF16 = jnp.bfloat16
CHUNK = 16
HIGHEST = lax.Precision.HIGHEST

V_GAIN, V_BIAS, V_QV, V_OUT, V_DOWN, V_UP = 0, 2, 4, 6, 7, 8
V_ROWS = 16


def dot(a, b):
    return lax.dot_general(a, b, (((1,), (0,)), ((), ())), preferred_element_type=F32)


def dot_t(a, b):
    return lax.dot_general(a, b, (((1,), (1,)), ((), ())), preferred_element_type=F32)


def t_dot(a, b):
    return lax.dot_general(a, b, (((0,), (0,)), ((), ())), preferred_element_type=F32)


def exact_dot(a, b, dims):
    return lax.dot_general(a, b, (dims, ((), ())), precision=HIGHEST, preferred_element_type=F32)


def when(condition):
    return pl.when(condition)


def scratch_of(half, per_row, width, hidden, images):
    tall = images * ROWS
    dma = pltpu.SemaphoreType.DMA
    vm = pltpu.VMEM
    return dict(
        wa=vm((LAYERS, D, 4 * width), BF16),
        wf=vm((LAYERS, D, 2 * hidden), BF16),
        ga=vm((D, 4 * width), BF16),
        gf=vm((D, 2 * hidden), BF16),
        pa=vm((half, per_row, 4 * width), BF16),
        pf=vm((half, per_row, 2 * hidden), BF16),
        ca=vm((half, per_row, 4 * width), BF16),
        cf=vm((half, per_row, 2 * hidden), BF16),
        x=vm((2, tall, D), BF16),
        e=vm((2 * LAYERS, tall, D), BF16),
        act=vm((2 * LAYERS, tall, D), BF16),
        q=vm((LAYERS, tall, width), BF16),
        k=vm((LAYERS, images * KEYS, width), BF16),
        v=vm((LAYERS, images * KEYS, width), BF16),
        o=vm((LAYERS, tall, width), BF16),
        prob=vm((LAYERS * images * (width // HEAD_DIM), ROWS, KEYS), F32),
        slope=vm((LAYERS, tall, hidden), F32),
        u=vm((LAYERS, tall, hidden), BF16),
        n=vm((2 * LAYERS, tall, width), F32),
        spread=vm((2 * LAYERS, tall, 1), F32),
        centre=vm((tall, 1), F32),
        r=vm((tall, width), F32),
        g=vm((tall, width), F32),
        f=vm((tall, hidden), BF16),
        d=vm((tall, 3 * width), BF16),
        do=vm((ROWS, width), BF16),
        tmp=vm((ROWS, width), F32),
        stage=vm((2, images, 3, ROWS, width), BF16),
        slot=vm((2, images, 4, ROWS, width), BF16),
        held=vm((images, 2, ROWS, width), F32),
        own=vm((2, images, ROWS, width), F32),
        vs=vm((2, KEYS, 128), F32),
        ts=vm((images, 8, KEYS), F32),
        tr=vm((images, 3, 8, KEYS), F32),
        gn=vm((4, 8, width), F32),
        sv=vm((LAYERS, V_ROWS, width), F32),
        rv=vm((LAYERS, 2 * half, V_ROWS, width), F32),
        ag_s=dma((4, images, 4)),
        ag_r=dma((4, images, 3)),
        rs_s=dma((2, images, 3)),
        rs_r=dma((2, images, 4)),
        t_s=dma((images, 3)),
        t_r=dma((images, 3)),
        gn_s=dma((3,)),
        gn_r=dma((3,)),
        w_l=dma((LAYERS, 2)),
        w_s=dma((LAYERS, 2, half + 1)),
        w_r=dma((LAYERS, 2, half)),
        w_f=dma((LAYERS, 2, half)),
        w_g=dma((LAYERS, 2, half)),
        p_s=dma((2, half)),
        p_r=dma((2, half)),
        c_s=dma((2, half)),
        c_r=dma((2, half)),
        v_s=dma((LAYERS, 2 * half)),
        v_r=dma((LAYERS, 2 * half)),
    )


IN_NAMES = ("x_in", "cot_in", "gb_in", "bq_in", "bo_in", "bu_in", "bd_in", "wa_in", "wf_in")
OUT_NAMES = ("out", "gin", "gwa", "gwf", "gv")


def kernel(wide, images, width, hidden, names, *refs):
    R = dict(zip(names, refs))
    half = wide // 2
    per_row = D // wide
    heads = width // HEAD_DIM
    w = lax.axis_index("wide")
    z = lax.axis_index("narrow")
    upper = z // 2
    mate = z + 1 - 2 * (z % 2)
    oi = 2 - upper
    oo = 3 * (1 - upper)
    inner_n = (z + upper) % 2
    inner = inner_n == 1
    outer = inner_n == 0
    far = 2 - inner_n
    par = w % 2
    mine = w // 2
    partner = w + 1 - 2 * par

    def rows(i):
        return pl.ds(i * ROWS, ROWS)

    def cols(j):
        return pl.ds(pl.multiple_of(j * width, 128), width)

    def block_rows(j):
        return pl.ds(pl.multiple_of(j * width, 128), width)

    def wrows(j):
        return pl.ds(pl.multiple_of(j * per_row, per_row), per_row)

    def remote(src, dst, s, r, wide_id, narrow_id):
        return pltpu.make_async_remote_copy(
            src_ref=src, dst_ref=dst, send_sem=s, recv_sem=r,
            device_id=(wide_id, narrow_id), device_id_type=MESH,
        )

    def chunks(count, body):
        lax.fori_loop(0, count // CHUNK, lambda c, _: (body(c * CHUNK), 0)[1], 0)

    def at(i, start, size=CHUNK):
        return pl.ds(pl.multiple_of(i * ROWS + start, CHUNK), size)

    def ag_copy(buf, kind, i, block, s, r, to):
        part = buf.at[rows(i), cols(block)]
        return remote(part, part, R["ag_s"].at[kind, i, s], R["ag_r"].at[kind, i, r], w, to)

    def ag_start(buf, kind, i):
        ag_copy(buf, kind, i, z, 0, 0, mate).start()
        ag_copy(buf, kind, i, z, 1, far, oi).start()

    def ag_relay(buf, kind, i):
        @when(inner)
        def _():
            ag_copy(buf, kind, i, oi, 2, 1, mate).wait_recv()
            ag_copy(buf, kind, i, oi, 2, 1, mate).start()
            ag_copy(buf, kind, i, oo, 3, 2, mate).wait_recv()
            ag_copy(buf, kind, i, oo, 3, 2, mate).start()

    def ag_finish(buf, kind, i):
        ag_copy(buf, kind, i, mate, 0, 0, mate).wait_recv()

        @when(outer)
        def _():
            ag_copy(buf, kind, i, oi, 2, 1, mate).wait_recv()
            ag_copy(buf, kind, i, oo, 3, 2, mate).wait_recv()

    def ag_drain(buf, kind, i):
        ag_copy(buf, kind, i, z, 0, 0, mate).wait_send()
        ag_copy(buf, kind, i, z, 1, far, oi).wait_send()

        @when(inner)
        def _():
            ag_copy(buf, kind, i, oi, 2, 1, mate).wait_send()
            ag_copy(buf, kind, i, oo, 3, 2, mate).wait_send()

    def rs_copy(bank, i, q, slot, to):
        return remote(
            R["stage"].at[bank, i, q], R["slot"].at[bank, i, slot],
            R["rs_s"].at[bank, i, q], R["rs_r"].at[bank, i, slot], w, to,
        )

    def rs_blocks(bank, i, block):
        for q, to in ((0, oo), (1, oi)):
            y = block(to)

            @when(outer)
            def _():
                R["stage"][bank, i, q] = y.astype(BF16)
                rs_copy(bank, i, q, q, mate).start()

            @when(inner)
            def _():
                R["held"][i, q] = y

        R["stage"][bank, i, 2] = block(mate).astype(BF16)
        rs_copy(bank, i, 2, 2, mate).start()
        R["own"][bank, i] = block(z)

    def rs_relay(bank, i):
        @when(inner)
        def _():
            for q, to in ((0, oo), (1, oi)):
                rs_copy(bank, i, q, q, mate).wait_recv()

                def body(c):
                    part = pl.ds(pl.multiple_of(c, CHUNK), CHUNK)
                    total = R["held"][i, q, part] + R["slot"][bank, i, q, part].astype(F32)
                    R["stage"][bank, i, q, part] = total.astype(BF16)

                chunks(ROWS, body)
                rs_copy(bank, i, q, 3, to).start()

    def rs_wait(bank, i):
        rs_copy(bank, i, 2, 2, mate).wait_recv()
        rs_copy(bank, i, 0, 3, mate).wait_recv()
        for q in range(3):
            rs_copy(bank, i, q, 2, mate).wait_send()

    def rs_sum(bank, i, part):
        slots = R["slot"]
        return (
            R["own"][bank, i, part]
            + slots[bank, i, 2, part].astype(F32)
            + slots[bank, i, 3, part].astype(F32)
        )

    def t_copy(i, q, r, to):
        return remote(
            R["ts"].at[i], R["tr"].at[i, r], R["t_s"].at[i, q], R["t_r"].at[i, r], w, to
        )

    def t_send(i):
        lane = lax.broadcasted_iota(jnp.int32, (8, 128), 0)
        first = jnp.where(lane < 4, 1.0, 0.0).astype(F32)
        second = 1.0 - first
        R["ts"][i] = exact_dot(first, R["vs"][0], ((1,), (1,))) + exact_dot(
            second, R["vs"][1], ((1,), (1,))
        )
        t_copy(i, 0, 0, mate).start()
        t_copy(i, 1, far, oi).start()
        t_copy(i, 2, far, oo).start()

    def t_total(i):
        for q in range(3):
            t_copy(i, q, q, mate).wait_recv()
        for q in range(3):
            t_copy(i, q, q, mate).wait_send()
        total = (R["ts"][i] + R["tr"][i, 0]) + (R["tr"][i, 1] + R["tr"][i, 2])
        row = lax.broadcasted_iota(jnp.int32, (8, 128), 0)
        lane = lax.broadcasted_iota(jnp.int32, (8, 128), 1)
        pick = ((row == 0) & (lane < 64)) | ((row == 4) & (lane >= 64))
        back = exact_dot(total, jnp.where(pick, 1.0, 0.0).astype(F32), ((0,), (0,)))
        R["vs"][0] = back

    def weights(piece):
        return (R["wa"], R["wa_in"]) if piece == 0 else (R["wf"], R["wf_in"])

    def w_local(l, piece):
        full, shard = weights(piece)
        return pltpu.make_async_copy(shard.at[l], full.at[l, wrows(w)], R["w_l"].at[l, piece])

    def w_send(l, piece, s, to):
        full, shard = weights(piece)
        return remote(
            shard.at[l], full.at[l, wrows(w)],
            R["w_s"].at[l, piece, s], R["w_r"].at[l, piece, mine], to, z,
        )

    def w_cross(l, piece, k):
        full, _ = weights(piece)
        part = full.at[l, wrows(2 * k + par)]
        return remote(
            part, part, R["w_g"].at[l, piece, k], R["w_f"].at[l, piece, k], partner, z
        )

    def w_start(l, piece):
        full, shard = weights(piece)
        for j in range(1, half):
            k = (mine + j) % half
            w_send(l, piece, j - 1, 2 * k + par).start()
        remote(
            shard.at[l], full.at[l, wrows(w)],
            R["w_s"].at[l, piece, half - 1], R["w_f"].at[l, piece, mine], partner, z,
        ).start()
        w_local(l, piece).start()

    def w_relay(l, piece):
        full, shard = weights(piece)
        for j in range(1, half):
            k = (mine + j) % half
            remote(
                shard.at[l], full.at[l, wrows(2 * k + par)],
                R["w_s"].at[l, piece, 0], R["w_r"].at[l, piece, k], partner, z,
            ).wait_recv()
            w_cross(l, piece, k).start()

    def w_finish(l, piece):
        full, shard = weights(piece)
        for j in range(half):
            k = (mine + j) % half
            part = full.at[l, wrows(2 * k + 1 - par)]
            remote(
                part, part, R["w_g"].at[l, piece, k], R["w_f"].at[l, piece, k], partner, z
            ).wait_recv()
        w_local(l, piece).wait()
        for s in range(half):
            w_send(l, piece, s, partner).wait_send()
        for j in range(1, half):
            w_cross(l, piece, (mine + j) % half).wait_send()

    def grads(piece):
        if piece == 0:
            return R["ga"], R["pa"], R["ca"], R["gwa"]
        return R["gf"], R["pf"], R["cf"], R["gwf"]

    def p_copy(piece, k):
        full, theirs, _, _ = grads(piece)
        return remote(
            full.at[wrows(2 * k + 1 - par)], theirs.at[k],
            R["p_s"].at[piece, k], R["p_r"].at[piece, k], partner, z,
        )

    def c_copy(piece, k, source):
        full, _, came, _ = grads(piece)
        return remote(
            full.at[wrows(2 * k + par)], came.at[source],
            R["c_s"].at[piece, k], R["c_r"].at[piece, source], 2 * k + par, z,
        )

    def g_start(piece):
        for k in range(half):
            p_copy(piece, k).start()

    def g_mid(piece):
        full, theirs, _, _ = grads(piece)
        for j in range(1, half + 1):
            k = (mine + j) % half
            p_copy(piece, k).wait_recv()

            def body(c):
                here = pl.ds(pl.multiple_of((2 * k + par) * per_row + c, CHUNK), CHUNK)
                total = full[here].astype(F32) + theirs[
                    k, pl.ds(pl.multiple_of(c, CHUNK), CHUNK)
                ].astype(F32)
                full[here] = total.astype(BF16)

            chunks(per_row, body)
            if j < half:
                c_copy(piece, k, mine).start()

    def g_end(l, piece):
        full, _, came, result = grads(piece)
        for j in range(1, half):
            k = (mine + j) % half
            c_copy(piece, k, k).wait_recv()

        def body(c):
            here = pl.ds(pl.multiple_of(w * per_row + c, CHUNK), CHUNK)
            part = pl.ds(pl.multiple_of(c, CHUNK), CHUNK)
            total = full[here].astype(F32)
            for j in range(1, half):
                total = total + came[(mine + j) % half, part].astype(F32)
            result[l, part] = total

        chunks(per_row, body)
        for k in range(half):
            p_copy(piece, k).wait_send()
        for j in range(1, half):
            c_copy(piece, (mine + j) % half, mine).wait_send()

    def v_copy(l, j, source):
        to = (w + j) % wide
        return remote(
            R["sv"].at[l], R["rv"].at[l, source],
            R["v_s"].at[l, j], R["v_r"].at[l, source], to, z,
        )

    def v_start(l):
        for j in range(1, wide):
            v_copy(l, j, w).start()

    def v_end(l):
        total = R["sv"][l]
        for j in range(1, wide):
            source = (w + j) % wide
            v_copy(l, j, source).wait_recv()
            total = total + R["rv"][l, source]
        R["gv"][l] = total
        for j in range(1, wide):
            v_copy(l, j, w).wait_send()

    def norm_in(buf, l, branch, i):
        at_norm = 2 * l + branch
        scale = [R["gn"][j, pl.ds(2 * l + branch, 1)] for j in range(4)]
        shift = [R["gn"][j, pl.ds(4 + 2 * l + branch, 1)] for j in range(4)]
        scale = jnp.concatenate(scale, axis=1)
        shift = jnp.concatenate(shift, axis=1)

        def body(c):
            here = at(i, c)
            raw = buf[here, :].astype(F32)
            mean = jnp.sum(raw, axis=1, keepdims=True) * (1.0 / D)
            square = jnp.sum(raw * raw, axis=1, keepdims=True) * (1.0 / D)
            s = lax.rsqrt(square - mean * mean + EPS)
            R["act"][at_norm, here] = ((raw - mean) * s * scale + shift).astype(BF16)
            centre = R["centre"][here] + mean
            R["centre"][here] = centre
            R["spread"][at_norm, here] = s
            R["n"][at_norm, here] = (R["r"][here] - centre) * s

        chunks(ROWS, body)

    def norm_back(bank, l, branch, i, v_out_row):
        at_norm = 2 * l + branch
        scale = R["gn"][z, pl.ds(2 * l + branch, 1)]
        rs_wait(bank, i)
        t_total(i)

        def body(c, carry):
            gain_sum, bias_sum, g_sum = carry
            c = c * CHUNK
            here = at(i, c)
            part = pl.ds(pl.multiple_of(c, CHUNK), CHUNK)
            upstream = rs_sum(bank, i, part)
            normed = R["n"][at_norm, here]
            first = R["vs"][0, part, 0:1] * (1.0 / D)
            second = R["vs"][0, part, 64:65] * (1.0 / D)
            grown = R["g"][here] + (upstream * scale - first - normed * second) * R["spread"][
                at_norm, here
            ]
            R["g"][here] = grown
            gain_sum = gain_sum + jnp.sum(upstream * normed, axis=0, keepdims=True)
            bias_sum = bias_sum + jnp.sum(upstream, axis=0, keepdims=True)
            g_sum = g_sum + jnp.sum(grown, axis=0, keepdims=True)
            return gain_sum, bias_sum, g_sum

        zero = jnp.zeros((1, width), F32)
        gain_sum, bias_sum, g_sum = lax.fori_loop(0, ROWS // CHUNK, body, (zero, zero, zero))
        small_add(l, V_GAIN + branch, gain_sum)
        small_add(l, V_BIAS + branch, bias_sum)
        if v_out_row is not None:
            small_add(l, v_out_row, g_sum)

    def small_add(l, row, value):
        R["sv"][l, row : row + 1] = R["sv"][l, row : row + 1] + value

    def send_sums(at_norm, i, block_of):
        R["vs"][0, 0:ROWS] = jnp.zeros((ROWS, 128), F32)
        R["vs"][1, 0:ROWS] = jnp.zeros((ROWS, 128), F32)
        l, branch = at_norm

        def block(j):
            y = block_of(j)
            R["tmp"][...] = y
            scale = R["gn"][j, pl.ds(2 * l + branch, 1)]
            shift = R["gn"][j, pl.ds(4 + 2 * l + branch, 1)]

            def body(c):
                part = pl.ds(pl.multiple_of(c, CHUNK), CHUNK)
                value = R["tmp"][part]
                normed = R["act"][2 * l + branch, at(i, c), cols(j)].astype(F32) - shift
                first = value * scale
                second = value * normed
                for m in range(width // 128):
                    lanes = slice(m * 128, (m + 1) * 128)
                    R["vs"][0, part] = R["vs"][0, part] + first[:, lanes]
                    R["vs"][1, part] = R["vs"][1, part] + second[:, lanes]

            chunks(ROWS, body)
            return R["tmp"][...]

        return block

    def attention(l, i):
        keys = pl.ds(i * KEYS, KEYS)
        column = lax.broadcasted_iota(jnp.int32, (ROWS, KEYS), 1)
        for h in range(heads):
            lanes = slice(h * HEAD_DIM, (h + 1) * HEAD_DIM)
            scores = dot_t(R["q"][l, rows(i), lanes], R["k"][l, keys, lanes]) * (
                1.0 / math.sqrt(HEAD_DIM)
            )
            scores = jnp.where(column < SEQ, scores, -jnp.inf)
            top = jnp.max(scores, axis=1, keepdims=True)
            grown = jnp.exp(scores - top)
            prob = grown / jnp.sum(grown, axis=1, keepdims=True)
            R["prob"][(l * images + i) * heads + h] = prob
            R["o"][l, rows(i), lanes] = dot(prob.astype(BF16), R["v"][l, keys, lanes]).astype(BF16)

    def f1(l, i):
        buf = R["x"].at[0]
        ag_finish(buf, 0, i)
        norm_in(buf, l, 0, i)
        act = R["act"].at[2 * l, rows(i)]
        kept = pl.ds(i * KEYS, ROWS)
        bq = R["bq_in"][pl.ds(2 * l, 1)]
        bv = R["bq_in"][pl.ds(2 * l + 1, 1)]
        R["q"][l, rows(i)] = (dot(act[...], R["wa"][l, :, 0:width]) + bq).astype(BF16)
        R["k"][l, kept] = dot(act[...], R["wa"][l, :, width : 2 * width]).astype(BF16)
        R["v"][l, kept] = (dot(act[...], R["wa"][l, :, 2 * width : 3 * width]) + bv).astype(BF16)
        attention(l, i)

        def block(j):
            return dot_t(R["o"][l, rows(i)], R["wa"][l, block_rows(j), 3 * width : 4 * width])

        rs_blocks(0, i, block)

    def f2(l, i):
        buf = R["x"].at[1]
        ag_finish(buf, 1, i)
        norm_in(buf, l, 1, i)

        def body(b, _):
            lanes = cols(b)
            pre = dot(R["act"][2 * l + 1, rows(i)], R["wf"][l, :, lanes])
            pre = pre + R["bu_in"][pl.ds(l, 1), lanes]
            cdf = 0.5 * (1.0 + lax.erf(pre * 0.7071067811865476))
            R["u"][l, rows(i), lanes] = (pre * cdf).astype(BF16)
            R["slope"][l, rows(i), lanes] = (
                cdf + pre * jnp.exp(-0.5 * pre * pre) * 0.3989422804014327
            )
            return 0

        lax.fori_loop(0, hidden // width, body, 0)

        def block(j):
            return dot_t(R["u"][l, rows(i)], R["wf"][l, block_rows(j), hidden : 2 * hidden])

        rs_blocks(1, i, block)

    def residual(bank, i, bias):
        rs_wait(bank, i)

        def body(c):
            here = at(i, c)
            part = pl.ds(pl.multiple_of(c, CHUNK), CHUNK)
            R["r"][here] = R["r"][here] + (rs_sum(bank, i, part) + bias)

        chunks(ROWS, body)

    def send_residual(kind, i):
        buf = R["x"].at[kind]

        def body(c):
            here = at(i, c)
            buf[here, cols(z)] = (R["r"][here] - R["centre"][here]).astype(BF16)

        chunks(ROWS, body)
        ag_start(buf, kind, i)

    def post_f1(l, i):
        ag_drain(R["x"].at[0], 0, i)
        residual(0, i, R["bo_in"][pl.ds(l, 1)])
        send_residual(1, i)

    def post_f2(l, i, last):
        ag_drain(R["x"].at[1], 1, i)
        residual(1, i, R["bd_in"][pl.ds(l, 1)])
        if last:
            R["out"][rows(i)] = R["r"][rows(i)]
        else:
            send_residual(0, i)

    def send_grad(slot, kind, i):
        buf = R["e"].at[slot]

        def body(c):
            here = at(i, c)
            buf[here, cols(z)] = R["g"][here].astype(BF16)

        chunks(ROWS, body)
        ag_start(buf, kind, i)

    def b2(l, i):
        e = R["e"].at[2 * l + 1]
        ag_finish(e, 2, i)

        def body(b, _):
            lanes = cols(b)
            back = pl.ds(pl.multiple_of(hidden + b * width, 128), width)
            dz = dot(e[rows(i), :], R["wf"][l, :, back]) * R["slope"][l, rows(i), lanes]
            R["f"][rows(i), lanes] = dz.astype(BF16)
            row = pl.ds(V_UP + b, 1)
            R["sv"][l, row] = R["sv"][l, row] + jnp.sum(dz, axis=0, keepdims=True)
            return 0

        lax.fori_loop(0, hidden // width, body, 0)

        def block(j):
            return dot_t(R["f"][rows(i)], R["wf"][l, block_rows(j), 0:hidden])

        rs_blocks(0, i, send_sums((l, 1), i, block))
        t_send(i)

    def b1(l, i):
        e = R["e"].at[2 * l]
        ag_finish(e, 3, i)
        keys = pl.ds(i * KEYS, KEYS)
        R["do"][...] = dot(e[rows(i), :], R["wa"][l, :, 3 * width : 4 * width]).astype(BF16)
        for h in range(heads):
            lanes = slice(h * HEAD_DIM, (h + 1) * HEAD_DIM)
            prob = R["prob"][(l * images + i) * heads + h]
            do = R["do"][:, lanes]
            dv = t_dot(prob.astype(BF16), do)[0:ROWS]
            dp = dot_t(do, R["v"][l, keys, lanes])
            delta = jnp.sum(prob * dp, axis=1, keepdims=True)
            ds = (prob * (dp - delta) * (1.0 / math.sqrt(HEAD_DIM))).astype(BF16)
            dq = dot(ds, R["k"][l, keys, lanes])
            dk = t_dot(ds, R["q"][l, rows(i), lanes])[0:ROWS]
            for part, value in ((0, dq), (1, dk), (2, dv)):
                there = slice(part * width + h * HEAD_DIM, part * width + (h + 1) * HEAD_DIM)
                R["d"][rows(i), there] = value.astype(BF16)
            for row, value in ((V_QV, dq), (V_QV + 1, dv)):
                total = jnp.sum(value, axis=0, keepdims=True)
                R["sv"][l, row : row + 1, lanes] = R["sv"][l, row : row + 1, lanes] + total

        def block(j):
            return dot_t(R["d"][rows(i)], R["wa"][l, block_rows(j), 0 : 3 * width])

        rs_blocks(1, i, send_sums((l, 0), i, block))
        t_send(i)

    def add_down(l, i):
        def body(c, total):
            return total + jnp.sum(R["g"][at(i, c * CHUNK)], axis=0, keepdims=True)

        total = lax.fori_loop(0, ROWS // CHUNK, body, jnp.zeros((1, width), F32))
        small_add(l, V_DOWN, total)

    def post_b2(l, i):
        add_down(l, i)
        ag_drain(R["e"].at[2 * l + 1], 2, i)
        norm_back(0, l, 1, i, V_OUT)
        send_grad(2 * l, 3, i)

    def post_b1(l, i):
        ag_drain(R["e"].at[2 * l], 3, i)
        norm_back(1, l, 0, i, None)

        @when(l > 0)
        def _():
            send_grad(2 * l - 1, 2, i)

        @when(l == 0)
        def _():
            R["gin"][rows(i)] = R["g"][rows(i)]

    def grad_ffn(l, first, last):
        def body(b, _):
            lanes = pl.ds(pl.multiple_of(b * 256, 256), 256)
            up = t_dot(R["act"][2 * l + 1, :, lanes], R["f"][...])
            R["gf"][lanes, 0:hidden] = up.astype(BF16)
            down = t_dot(R["e"][2 * l + 1, :, lanes], R["u"][l])
            R["gf"][lanes, hidden : 2 * hidden] = down.astype(BF16)
            return 0

        lax.fori_loop(first, last, body, 0)

    def grad_attention(l, first, last):
        def body(b, _):
            lanes = pl.ds(pl.multiple_of(b * 256, 256), 256)
            qkv = t_dot(R["act"][2 * l, :, lanes], R["d"][...])
            R["ga"][lanes, 0 : 3 * width] = qkv.astype(BF16)
            out = t_dot(R["e"][2 * l, :, lanes], R["o"][l])
            R["ga"][lanes, 3 * width : 4 * width] = out.astype(BF16)
            return 0

        lax.fori_loop(first, last, body, 0)

    barrier = pltpu.get_barrier_semaphore()
    for j in range(1, 4):
        pl.semaphore_signal(barrier, 1, device_id=(w, (z + j) % 4), device_id_type=MESH)
    for j in range(1, wide):
        pl.semaphore_signal(barrier, 1, device_id=((w + j) % wide, z), device_id_type=MESH)
    pl.semaphore_wait(barrier, 3 + wide - 1)

    w_start(0, 0)
    image = range(images)
    for i in image:
        R["x"][0, rows(i), cols(z)] = R["x_in"][rows(i)]
        ag_start(R["x"].at[0], 0, i)

    def gn_copy(q, r, to):
        return remote(R["gb_in"], R["gn"].at[z], R["gn_s"].at[q], R["gn_r"].at[r], w, to)

    gn_copy(0, 0, mate).start()
    gn_copy(1, far, oi).start()
    gn_copy(2, far, oo).start()
    R["gn"][z] = R["gb_in"][...]
    R["r"][...] = R["x_in"][...].astype(F32)
    R["g"][...] = R["cot_in"][...].astype(F32)
    R["centre"][...] = jnp.zeros_like(R["centre"])
    R["sv"][...] = jnp.zeros_like(R["sv"])
    R["vs"][...] = jnp.zeros_like(R["vs"])
    for name in ("k", "v"):
        for i in image:
            empty = jnp.zeros((LAYERS, KEYS - ROWS, width), BF16)
            R[name][:, i * KEYS + ROWS : (i + 1) * KEYS] = empty
    for i in image:
        ag_relay(R["x"].at[0], 0, i)
    last_e = R["e"].at[2 * LAYERS - 1]
    for i in image:
        last_e[rows(i), cols(z)] = R["cot_in"][rows(i)]
        ag_start(last_e, 2, i)
    for q in range(3):
        gn_copy(q, q, mate).wait_recv()
    for q in range(3):
        gn_copy(q, q, mate).wait_send()
    w_relay(0, 0)
    w_finish(0, 0)
    w_start(0, 1)
    for i in image:
        ag_relay(last_e, 2, i)

    def forward(l, _):
        f1(l, 0)

        @when(l > 0)
        def _():
            ag_relay(R["x"].at[0], 0, 1)

        rs_relay(0, 0)
        f1(l, 1)
        post_f1(l, 0)
        w_relay(l, 1)
        rs_relay(0, 1)
        ag_relay(R["x"].at[1], 1, 0)
        post_f1(l, 1)
        w_finish(l, 1)

        @when(l < LAYERS - 1)
        def _():
            w_start(l + 1, 0)

        f2(l, 0)
        ag_relay(R["x"].at[1], 1, 1)
        rs_relay(1, 0)
        f2(l, 1)

        @when(l < LAYERS - 1)
        def _():
            w_relay(l + 1, 0)
            post_f2(l, 0, False)
            rs_relay(1, 1)
            ag_relay(R["x"].at[0], 0, 0)
            post_f2(l, 1, False)
            w_finish(l + 1, 0)
            w_start(l + 1, 1)

        return 0

    lax.fori_loop(0, LAYERS, forward, 0)

    def backward(step, _):
        l = LAYERS - 1 - step
        top = l == LAYERS - 1
        e2 = R["e"].at[2 * l + 1]
        e1 = R["e"].at[2 * l]
        b2(l, 0)

        @when(top)
        def _():
            rs_relay(1, 1)

        @when(l < LAYERS - 1)
        def _():
            ag_relay(e2, 2, 1)

        rs_relay(0, 0)
        b2(l, 1)

        @when(top)
        def _():
            post_f2(l, 0, True)
            post_f2(l, 1, True)

        post_b2(l, 0)
        grad_ffn(l, 0, 2)
        rs_relay(0, 1)
        ag_relay(e1, 3, 0)
        post_b2(l, 1)
        grad_ffn(l, 2, 4)
        g_start(1)
        b1(l, 0)
        ag_relay(e1, 3, 1)
        rs_relay(1, 0)

        @when(l < LAYERS - 1)
        def _():
            g_end(l + 1, 0)

        g_mid(1)
        b1(l, 1)
        post_b1(l, 0)
        grad_attention(l, 0, 4)
        g_start(0)
        rs_relay(1, 1)

        @when(l > 0)
        def _():
            ag_relay(R["e"].at[2 * l - 1], 2, 0)

        post_b1(l, 1)
        g_end(l, 1)
        g_mid(0)
        v_start(l)
        return 0

    lax.fori_loop(0, LAYERS, backward, 0)
    for l in range(LAYERS):
        v_end(l)
    g_end(0, 0)


def body(wide, inputs, norm_gain, norm_bias, w_qkv, b_qv, w_out, b_out, w_up, b_up, w_down, b_down, cotangent):
    tokens, width = inputs.shape
    images = tokens // SEQ
    hidden = w_up.shape[2]
    per_row = w_up.shape[1]
    half = wide // 2
    tall = images * ROWS

    def padded(matrix):
        shaped = matrix.reshape(images, SEQ, width)
        return jnp.pad(shaped, ((0, 0), (0, ROWS - SEQ), (0, 0))).reshape(tall, width)

    def unpadded(matrix):
        return matrix.reshape(images, ROWS, width)[:, :SEQ].reshape(tokens, width)

    wa = jnp.concatenate(
        [w_qkv.reshape(LAYERS, per_row, 3 * width), w_out.transpose(0, 2, 1)], axis=2
    )
    wf = jnp.concatenate([w_up, w_down.transpose(0, 2, 1)], axis=2)
    gb = jnp.concatenate(
        [norm_gain.reshape(2 * LAYERS, width), norm_bias.reshape(2 * LAYERS, width)], axis=0
    )
    scratch = scratch_of(half, per_row, width, hidden, images)
    names = IN_NAMES + OUT_NAMES + tuple(scratch)
    vmem = pl.BlockSpec(memory_space=pltpu.VMEM)
    anywhere = pl.BlockSpec(memory_space=pl.ANY)
    out, gin, gwa, gwf, gv = pl.pallas_call(
        functools.partial(kernel, wide, images, width, hidden, names),
        out_shape=(
            jax.ShapeDtypeStruct((tall, width), F32),
            jax.ShapeDtypeStruct((tall, width), F32),
            jax.ShapeDtypeStruct((LAYERS, per_row, 4 * width), F32),
            jax.ShapeDtypeStruct((LAYERS, per_row, 2 * hidden), F32),
            jax.ShapeDtypeStruct((LAYERS, V_ROWS, width), F32),
        ),
        in_specs=[vmem] * 7 + [anywhere] * 2,
        out_specs=(vmem,) * 5,
        scratch_shapes=list(scratch.values()),
        compiler_params=pltpu.CompilerParams(
            collective_id=0, has_side_effects=True, vmem_limit_bytes=67043328
        ),
        name="encoder_step",
    )(
        padded(inputs), padded(cotangent), gb, b_qv.reshape(2 * LAYERS, width), b_out, b_up,
        b_down, wa, wf,
    )
    return (
        unpadded(out),
        unpadded(gin),
        gv[:, V_GAIN : V_GAIN + 2],
        gv[:, V_BIAS : V_BIAS + 2],
        gwa[:, :, : 3 * width].reshape(LAYERS, per_row, 3, width),
        gv[:, V_QV : V_QV + 2],
        gwa[:, :, 3 * width :].transpose(0, 2, 1),
        gv[:, V_OUT],
        gwf[:, :, :hidden],
        gv[:, V_UP : V_UP + hidden // width].reshape(LAYERS, hidden),
        gwf[:, :, hidden:].transpose(0, 2, 1),
        gv[:, V_DOWN],
    )


def solution(mesh):
    rows = P("wide", "narrow")
    vector2 = P(None, None, "narrow")
    vector = P(None, "narrow")
    down_cols = P(None, "narrow", "wide")
    up_rows = P(None, "wide", "narrow")
    qkv = P(None, "wide", None, "narrow")
    return jax.shard_map(
        functools.partial(body, mesh.shape["wide"]),
        mesh=mesh,
        in_specs=(
            rows, vector2, vector2, qkv, vector2, down_cols, vector, up_rows, vector, down_cols,
            vector, rows,
        ),
        out_specs=(
            rows, rows, vector2, vector2, qkv, vector2, down_cols, vector, up_rows, vector,
            down_cols, vector,
        ),
        check_vma=False,
    )
```

time: 873 us -> 301 us (0.34)
  waiting for transfers between devices: 381 us -> 0 us
  blocking collectives: 281 us -> 0 us
  Pallas kernels: 0 us -> 274 us
  matrix products: 84.9 us -> 0 us
  local copies, waits for them, and re-layouts: 67 us -> 18.1 us
  other arithmetic: 33.6 us -> 2.52 us
  between operations: 15.6 us -> 0.78 us
    reduce_scatter x10 -> x0, waiting for transfers between devices: 299 us -> none  [the longest x4 137 us: sum_input_grad(): lax.psum_scatter(partial_sum, 'narrow', scatter_dimension=1, tiled=True)]
    pallas_call x0 -> x1, Pallas kernels: none -> 274 us  [body(): pl.pallas_call(functools.partial(kernel, wide, images, width, hidden, nam...]
    all_gather x10 -> x0, blocking collectives: 174 us -> none  [the longest x4 81.7 us: gather_grad(): lax.all_gather(upstream.astype(jnp.bfloat16), 'narrow', axis=1, tiled=True)]
    psum x9 -> x0, blocking collectives: 107 us -> none  [the longest x4 44.1 us: norm_forward(): lax.psum((jnp.sum(residual, axis=1), jnp.sum(residual * residual, axis=1)...]
    dot_general x36 -> x0, matrix products: 84.9 us -> none  [the longest x8 21.3 us: times_transpose(): lax.dot_general(former, latter, (((1,), (1,)), ((), ())), preferred_eleme...]
    all_gather x6 -> x0, waiting for transfers between devices: 51 us -> none  [the longest x2 50.2 us: body(): lax.all_gather(w_down[number], 'wide', axis=1, tiled=True)]
    unnamed x174 -> x21, local copies, waits for them, and re-layouts: 40.1 us -> 5.95 us
    unnamed x20 -> x0, waiting for transfers between devices: 31.1 us -> none
  transfers between devices with their start and end apart: 18 -> 0, of which waited for: 14 -> 0; matrix products, arithmetic and copies ran while one was open for 11% -> 0% of each run, Pallas kernels for 0% -> 0%
where the time goes in v1:
time: 301 us; the launch traced here: 296 us
  Pallas kernels  274 us (91%)
  local copies, waits for them, and re-layouts  18.1 us (6%)
    pallas_call x1, Pallas kernels, body(): pl.pallas_call(functools.partial(kernel, wide, images, width, hidden, nam...  274 us

profile of v1, /device:TPU:0, one launch (start us, length us, event | category | flops | bytes accessed | tf_op | source)
XLA Modules:
  0.0 295.9 jit_solution(13140641949456152995)
XLA Ops:
  0.6 0.0 copy-start.4
  0.7 0.8 reshape.70
  1.4 0.7 reshape.71
  2.1 0.6 pad_maximum_fusion.2.refs_2_
  2.7 1.3 reshape.72.refs_3_
  4.0 1.0 copy.31
  5.0 0.0 copy-start.2
  5.0 1.0 reshape.66
  6.1 0.7 pad.7
  6.8 1.0 reshape.68
  7.7 0.0 copy-start.3
  7.8 0.7 pad.8
  8.5 0.0 copy-done.4
  8.5 0.2 copy.30
  8.7 0.2 copy.32
  8.9 0.9 pad_maximum_fusion.1.refs_7_
  9.7 0.0 copy-done.2
  9.7 0.2 copy.33
  9.9 0.0 copy-done.3
  10.0 1.1 pad_maximum_fusion.refs_8_
  11.0 274.4 %encoder_step.1 = (f32[416,256]{1,0:T(8,128)}, f32[416,256]{1,0:T(8,128)}, f32[2,128,1024]{2,1,0:T(8,128)}, f32[2,128,2048]{2,1,0:T(8,128)}, f32[2,16,256]{2,1,0:T(8,128)}) custom-call(bf16[416,256]{1,0:T(8,128)(2,1)} %bitcast.22, bf16[416,256]{1,0:T(8,128)(2,1)} %bitcast.23, f32[8,256]{1,0:T(8,128)} %pad_maximum_fusion.2.refs_2_, ...), custom_call_target="tpu_custom_call" | custom-call | tf_op jit(solution)/shard_map/encoder_step/pallas_call | solution.py:856
  285.5 0.0 copy-start.5
  285.5 0.0 copy-start.1
  285.5 1.1 slice.48
  286.6 0.8 reshape.75
  287.4 1.0 slice.49
  288.4 0.8 reshape.77
  289.2 0.0 copy-done.5
  289.2 0.6 copy_bitcast_fusion
  289.8 0.6 fusion.1
  290.4 0.6 copy.40
  291.0 0.0 copy-done.1
  291.1 0.1 slice.40
  291.1 0.3 copy.34
  291.4 0.0 copy-start
  291.4 1.1 copy.35
  292.5 0.8 copy.36
  293.4 0.0 copy-done
  293.4 1.2 slice_bitcast_fusion
  294.5 1.3 copy.37
  (3 shorter events, 0.0 us)
Async XLA Ops:
  0.6 7.8 %copy-start.4 = (bf16[2,128,3,256]{3,1,2,0:T(8,128)(2,1)S(1)}, bf16[2,128,3,256]{3,1,2,0:T(8,128)(2,1)}, u32[]{:S(2)}) copy-start(bf16[2,128,3,256]{3,1,2,0:T(8,128)(2,1)} %param.15) | copy-start | bytes 1179652
  5.0 4.7 %copy-start.2 = (bf16[2,1024,128]{2,1,0:T(8,128)(2,1)S(1)}, bf16[2,1024,128]{2,1,0:T(8,128)(2,1)}, u32[]{:S(2)}) copy-start(bf16[2,1024,128]{2,1,0:T(8,128)(2,1)} %param.21) | copy-start | bytes 1572868
  7.7 2.2 copy-start.3
  285.5 3.8 %copy-start.5 = (f32[2,16,256]{2,1,0:T(8,128)S(1)}, f32[2,16,256]{2,1,0:T(8,128)}, u32[]{:S(2)}) copy-start(f32[2,16,256]{2,1,0:T(8,128)} %get-tuple-element.19) | copy-start | bytes 98308
  285.5 5.6 %copy-start.1 = (f32[2,128,1024]{2,1,0:T(8,128)S(1)}, f32[2,128,1024]{2,1,0:T(8,128)}, u32[]{:S(2)}) copy-start(f32[2,128,1024]{2,1,0:T(8,128)} %get-tuple-element.20) | copy-start | bytes 3145732
  291.4 2.0 copy-start

commit v2 on v1

v2 whole, which is shorter than its diff:
```python
import functools
import math

import jax
import jax.numpy as jnp
from jax import lax
from jax.experimental import pallas as pl
from jax.experimental.pallas import tpu as pltpu
from jax.sharding import PartitionSpec as P

D = 1024
HEAD_DIM = 64
SEQ = 197
LAYERS = 2
EPS = 1e-06
ROWS = 208
KEYS = 256
MESH = pl.DeviceIdType.MESH
F32 = jnp.float32
BF16 = jnp.bfloat16
CHUNK = 16
HIGHEST = lax.Precision.HIGHEST

V_GAIN, V_BIAS, V_OUT, V_DOWN, V_QV, V_UP = 0, 2, 4, 5, 8, 10
V_ROWS = 16
G_GAIN, G_BIAS, G_OUT, G_DOWN = 0, 4, 8, 10
G_ROWS = 16


def dot(a, b):
    return lax.dot_general(a, b, (((1,), (0,)), ((), ())), preferred_element_type=F32)


def dot_t(a, b):
    return lax.dot_general(a, b, (((1,), (1,)), ((), ())), preferred_element_type=F32)


def t_dot(a, b):
    return lax.dot_general(a, b, (((0,), (0,)), ((), ())), preferred_element_type=F32)


def exact_dot(a, b, dims):
    return lax.dot_general(a, b, (dims, ((), ())), precision=HIGHEST, preferred_element_type=F32)


def when(condition):
    return pl.when(condition)


def scratch_of(half, per_row, width, hidden, images):
    tall = images * ROWS
    dma = pltpu.SemaphoreType.DMA
    vm = pltpu.VMEM
    return dict(
        wa=vm((LAYERS, D, 4 * width), BF16),
        wf=vm((LAYERS, D, 2 * hidden), BF16),
        ga=vm((D, 4 * width), BF16),
        gf=vm((D, 2 * hidden), BF16),
        pa=vm((LAYERS * half, per_row, 4 * width), BF16),
        pf=vm((half, per_row, 2 * hidden), BF16),
        ca=vm((LAYERS * half, per_row, 4 * width), BF16),
        cf=vm((half, per_row, 2 * hidden), BF16),
        e=vm((2 * LAYERS, tall, D), BF16),
        act=vm((2 * LAYERS, tall, D), BF16),
        q=vm((LAYERS, tall, width), BF16),
        k=vm((LAYERS, images * KEYS, width), BF16),
        v=vm((LAYERS, images * KEYS, width), BF16),
        o=vm((LAYERS, tall, width), BF16),
        prob=vm((LAYERS * images * (width // HEAD_DIM), ROWS, KEYS), F32),
        slope=vm((LAYERS, tall, hidden), F32),
        u=vm((LAYERS, tall, hidden), BF16),
        n=vm((2 * LAYERS, tall, 2 * width), F32),
        spread=vm((2 * LAYERS, tall, 1), F32),
        centre=vm((tall, 1), F32),
        r=vm((tall, 2 * width), F32),
        g=vm((tall, 2 * width), F32),
        f=vm((tall, hidden), BF16),
        d=vm((tall, 3 * width), BF16),
        do=vm((ROWS, width), BF16),
        tmp=vm((ROWS, width), F32),
        stage=vm((2, images, 4, ROWS, width), BF16),
        slot=vm((2, images, 6, ROWS, width), BF16),
        held=vm((images, 2, ROWS, width), F32),
        own=vm((2, images, 2, ROWS, width), F32),
        vs=vm((2, KEYS, 128), F32),
        ts=vm((images, 8, KEYS), F32),
        tr=vm((images, 3, 8, KEYS), F32),
        gb=vm((G_ROWS, width), F32),
        gn=vm((4, G_ROWS, width), F32),
        ra=vm((per_row, 4 * width), F32),
        rf=vm((per_row, 2 * hidden), F32),
        wo=vm((LAYERS, per_row, width), BF16),
        wd=vm((LAYERS, per_row, hidden), BF16),
        sh=vm((LAYERS, 2, 8, width), F32),
        sm=vm((LAYERS, 8, width), F32),
        sv=vm((LAYERS, V_ROWS, width), F32),
        rv=vm((LAYERS, 2 * half, V_ROWS, width), F32),
        a0_s=dma((2, images, 4)),
        a0_r=dma((2, images, 3)),
        ag_s=dma((4, images, 6)),
        ag_r=dma((4, images, 4)),
        rs_s=dma((2, images, 4)),
        rs_r=dma((2, images, 6)),
        t_s=dma((images, 2)),
        t_r=dma((images, 3)),
        gn_s=dma((3,)),
        gn_r=dma((3,)),
        sm_s=dma((LAYERS,)),
        sm_r=dma((LAYERS,)),
        fin_s=dma((2, images)),
        fin_r=dma((2, images)),
        w_l=dma((LAYERS, 4)),
        w_s=dma((LAYERS, 4, half)),
        w_r=dma((LAYERS, 4, half)),
        w_f=dma((LAYERS, 4, half)),
        w_g=dma((LAYERS, 4, half)),
        p_s=dma((2, half)),
        p_r=dma((LAYERS, 2, half)),
        c_s=dma((2, half)),
        c_r=dma((LAYERS, 2, half)),
        r_s=dma((LAYERS, 2)),
        v_s=dma((LAYERS, 2 * half)),
        v_r=dma((LAYERS, 2 * half)),
    )


IN_NAMES = (
    "x_in", "cot_in", "ng_in", "nb_in", "bq_in", "bo_in", "bu_in", "bd_in", "wo_in", "wd_in",
    "wq_in", "wu_in",
)
OUT_NAMES = ("out", "gin", "gwa", "gwf", "gv")


def kernel(wide, images, width, hidden, names, *refs):
    R = dict(zip(names, refs))
    R["x"] = R["e"].at[0:2]
    half = wide // 2
    per_row = D // wide
    heads = width // HEAD_DIM
    w = lax.axis_index("wide")
    z = lax.axis_index("narrow")
    upper = z // 2
    mate = z + 1 - 2 * (z % 2)
    oi = 2 - upper
    oo = 3 * (1 - upper)
    inner_n = (z + upper) % 2
    inner = inner_n == 1
    outer = inner_n == 0
    far = 2 - inner_n
    near_half = 2 * upper
    far_half = 2 - near_half
    inside = z % 2
    half_cols = pl.ds(pl.multiple_of(near_half * width, 128), 2 * width)
    par = w % 2
    mine = w // 2
    partner = w + 1 - 2 * par

    def rows(i):
        return pl.ds(i * ROWS, ROWS)

    def cols(j):
        return pl.ds(pl.multiple_of(j * width, 128), width)

    def block_rows(j):
        return pl.ds(pl.multiple_of(j * width, 128), width)

    def wrows(j):
        return pl.ds(pl.multiple_of(j * per_row, per_row), per_row)

    def remote(src, dst, s, r, wide_id, narrow_id):
        return pltpu.make_async_remote_copy(
            src_ref=src, dst_ref=dst, send_sem=s, recv_sem=r,
            device_id=(wide_id, narrow_id), device_id_type=MESH,
        )

    def chunks(count, body, unroll=False):
        lax.fori_loop(
            0, count // CHUNK, lambda c, _: (body(c * CHUNK), 0)[1], 0, unroll=unroll
        )

    def at(i, start, size=CHUNK):
        return pl.ds(pl.multiple_of(i * ROWS + start, CHUNK), size)

    def a0_copy(buf, kind, i, block, s, r, to):
        part = buf.at[rows(i), cols(block)]
        return remote(part, part, R["a0_s"].at[kind, i, s], R["a0_r"].at[kind, i, r], w, to)

    def a0_start(buf, kind, i):
        a0_copy(buf, kind, i, z, 0, 0, mate).start()
        a0_copy(buf, kind, i, z, 1, far, oi).start()

    def a0_relay(buf, kind, i):
        @when(inner)
        def _():
            for r, block in ((1, oi), (2, oo)):
                a0_copy(buf, kind, i, block, r + 1, r, mate).wait_recv()
                a0_copy(buf, kind, i, block, r + 1, r, mate).start()

    def a0_finish(buf, kind, i):
        a0_copy(buf, kind, i, mate, 0, 0, mate).wait_recv()

        @when(outer)
        def _():
            for r, block in ((1, oi), (2, oo)):
                a0_copy(buf, kind, i, block, r + 1, r, mate).wait_recv()

        a0_copy(buf, kind, i, z, 0, 0, mate).wait_send()
        a0_copy(buf, kind, i, z, 1, far, oi).wait_send()

        @when(inner)
        def _():
            for r, block in ((1, oi), (2, oo)):
                a0_copy(buf, kind, i, block, r + 1, r, mate).wait_send()

    def ag_copy(buf, kind, i, block, s, r, to):
        part = buf.at[rows(i), cols(block)]
        return remote(part, part, R["ag_s"].at[kind, i, s], R["ag_r"].at[kind, i, r], w, to)

    def ag_start(buf, kind, i):
        @when(inner)
        def _():
            for u in range(2):
                ag_copy(buf, kind, i, near_half + u, u, u, oi).start()
            for u in range(2):
                ag_copy(buf, kind, i, near_half + u, 2 + u, 2 + u, mate).start()

    def ag_relay(buf, kind, i):
        @when(inner)
        def _():
            for u in range(2):
                ag_copy(buf, kind, i, far_half + u, 4 + u, u, mate).wait_recv()
                ag_copy(buf, kind, i, far_half + u, 4 + u, u, mate).start()

    def ag_finish(buf, kind, i):
        @when(outer)
        def _():
            for u in range(2):
                ag_copy(buf, kind, i, near_half + u, 2 + u, 2 + u, mate).wait_recv()
            for u in range(2):
                ag_copy(buf, kind, i, far_half + u, 4 + u, u, mate).wait_recv()

    def ag_drain(buf, kind, i):
        @when(inner)
        def _():
            for u in range(2):
                ag_copy(buf, kind, i, near_half + u, u, u, oi).wait_send()
                ag_copy(buf, kind, i, near_half + u, 2 + u, 2 + u, mate).wait_send()
                ag_copy(buf, kind, i, far_half + u, 4 + u, u, mate).wait_send()

    def rs_copy(bank, i, q, slot, to):
        return remote(
            R["stage"].at[bank, i, q], R["slot"].at[bank, i, slot],
            R["rs_s"].at[bank, i, q], R["rs_r"].at[bank, i, slot], w, to,
        )

    def rs_blocks(bank, i, block):
        for q in range(4):
            y = block((far_half if q < 2 else near_half) + q % 2)

            @when(outer)
            def _():
                R["stage"][bank, i, q] = y.astype(BF16)
                rs_copy(bank, i, q, q, mate).start()

            @when(inner)
            def _():
                if q < 2:
                    R["held"][i, q] = y
                else:
                    R["own"][bank, i, q - 2] = y

    def rs_relay(bank, i):
        @when(inner)
        def _():
            for q in range(2):
                rs_copy(bank, i, q, q, mate).wait_recv()

                def body(c):
                    part = pl.ds(pl.multiple_of(c, CHUNK), CHUNK)
                    total = R["held"][i, q, part] + R["slot"][bank, i, q, part].astype(F32)
                    R["stage"][bank, i, q, part] = total.astype(BF16)

                chunks(ROWS, body, True)
                rs_copy(bank, i, q, 4 + q, oi).start()

    def rs_wait(bank, i):
        @when(inner)
        def _():
            for q in range(2, 4):
                rs_copy(bank, i, q, q, mate).wait_recv()
            for q in range(2):
                rs_copy(bank, i, q, 4 + q, oi).wait_recv()
            for q in range(2):
                rs_copy(bank, i, q, 4 + q, oi).wait_send()

        @when(outer)
        def _():
            for q in range(4):
                rs_copy(bank, i, q, q, mate).wait_send()

    def rs_sum(bank, i, part):
        slots = R["slot"]
        return jnp.concatenate(
            [
                R["own"][bank, i, u, part]
                + slots[bank, i, 2 + u, part].astype(F32)
                + slots[bank, i, 4 + u, part].astype(F32)
                for u in range(2)
            ],
            axis=1,
        )

    def near_row(row):
        return jnp.concatenate([R["gn"][near_half + u, row] for u in range(2)], axis=1)

    def t_copy(i, q, r, to):
        return remote(
            R["ts"].at[i], R["tr"].at[i, r], R["t_s"].at[i, q], R["t_r"].at[i, r], w, to
        )

    def t_send(i):
        lane = lax.broadcasted_iota(jnp.int32, (8, 128), 0)
        first = jnp.where(lane < 4, 1.0, 0.0).astype(F32)
        second = 1.0 - first
        R["ts"][i] = exact_dot(first, R["vs"][0], ((1,), (1,))) + exact_dot(
            second, R["vs"][1], ((1,), (1,))
        )
        @when(outer)
        def _():
            t_copy(i, 0, 0, mate).start()

        t_copy(i, 1, far, oi).start()

    def t_total(i):
        for q in range(3):
            t_copy(i, 0, q, mate).wait_recv()
        total = (R["ts"][i] + R["tr"][i, 0]) + (R["tr"][i, 1] + R["tr"][i, 2])
        row = lax.broadcasted_iota(jnp.int32, (8, 128), 0)
        lane = lax.broadcasted_iota(jnp.int32, (8, 128), 1)
        pick = ((row == 0) & (lane < 64)) | ((row == 4) & (lane >= 64))
        R["vs"][0] = exact_dot(total, jnp.where(pick, 1.0, 0.0).astype(F32), ((0,), (0,)))

    def t_drain(i):
        @when(outer)
        def _():
            t_copy(i, 0, 0, mate).wait_send()

        t_copy(i, 1, far, oi).wait_send()

    def weights(l, piece):
        if piece == 0:
            return R["wa"].at[l, :, 0 : 3 * width], R["wq_in"].at[l]
        if piece == 1:
            return R["wa"].at[l, :, 3 * width : 4 * width], R["wo"].at[l]
        if piece == 2:
            return R["wf"].at[l, :, 0:hidden], R["wu_in"].at[l]
        return R["wf"].at[l, :, hidden : 2 * hidden], R["wd"].at[l]

    def w_local(l, piece):
        full, shard = weights(l, piece)
        return pltpu.make_async_copy(shard, full.at[wrows(w)], R["w_l"].at[l, piece])

    def w_send(l, piece, s, to):
        full, shard = weights(l, piece)
        return remote(
            shard, full.at[wrows(w)], R["w_s"].at[l, piece, s], R["w_r"].at[l, piece, mine], to, z
        )

    def w_pair(l, piece):
        full, shard = weights(l, piece)
        return remote(
            shard, full.at[wrows(w)],
            R["w_s"].at[l, piece, half - 1], R["w_f"].at[l, piece, mine], partner, z,
        )

    def w_cross(l, piece, k, parity):
        full, _ = weights(l, piece)
        part = full.at[wrows(2 * k + parity)]
        return remote(
            part, part, R["w_g"].at[l, piece, k], R["w_f"].at[l, piece, k], partner, z
        )

    def w_start(l, piece):
        for j in range(1, half):
            w_send(l, piece, j - 1, 2 * ((mine + j) % half) + par).start()
        w_pair(l, piece).start()
        w_local(l, piece).start()

    def w_relay(l, piece):
        full, shard = weights(l, piece)
        for j in range(1, half):
            k = (mine + half - j) % half
            remote(
                shard, full.at[wrows(2 * k + par)],
                R["w_s"].at[l, piece, 0], R["w_r"].at[l, piece, k], partner, z,
            ).wait_recv()
            w_cross(l, piece, k, par).start()

    def w_finish(l, piece):
        for j in range(half):
            w_cross(l, piece, (mine + half - j) % half, 1 - par).wait_recv()
        w_local(l, piece).wait()
        for s in range(half - 1):
            w_send(l, piece, s, partner).wait_send()
        w_pair(l, piece).wait_send()
        for j in range(1, half):
            w_cross(l, piece, (mine + j) % half, par).wait_send()

    def grads(l, piece):
        if piece == 0:
            room = pl.ds(l * half, half)
            return R["ga"], R["pa"].at[room], R["ca"].at[room], R["ra"], R["gwa"].at[l]
        return R["gf"], R["pf"], R["cf"], R["rf"], R["gwf"].at[l]

    def p_copy(l, piece, k):
        full, theirs, _, _, _ = grads(l, piece)
        return remote(
            full.at[wrows(2 * k + 1 - par)], theirs.at[k],
            R["p_s"].at[piece, k], R["p_r"].at[l, piece, k], partner, z,
        )

    def c_copy(l, piece, k, source):
        full, _, came, _, _ = grads(l, piece)
        return remote(
            full.at[wrows(2 * k + par)], came.at[source],
            R["c_s"].at[piece, k], R["c_r"].at[l, piece, source], 2 * k + par, z,
        )

    def r_copy(l, piece):
        _, _, _, total, result = grads(l, piece)
        return pltpu.make_async_copy(total, result, R["r_s"].at[l, piece])

    def g_start(l, piece, b):
        pairs = half * 256 // D
        for k in range(pairs):
            p_copy(l, piece, b * pairs + k).start()

    def g_mid(l, piece):
        full, theirs, _, _, _ = grads(l, piece)
        for j in range(1, half + 1):
            k = (mine + j) % half
            p_copy(l, piece, k).wait_recv()

            def body(c):
                here = pl.ds(pl.multiple_of((2 * k + par) * per_row + c, CHUNK), CHUNK)
                total = full[here].astype(F32) + theirs[
                    k, pl.ds(pl.multiple_of(c, CHUNK), CHUNK)
                ].astype(F32)
                full[here] = total.astype(BF16)

            chunks(per_row, body)
            if j < half:
                c_copy(l, piece, k, mine).start()

    def g_end(l, piece):
        full, _, came, result, _ = grads(l, piece)
        for j in range(1, half):
            k = (mine + half - j) % half
            c_copy(l, piece, k, k).wait_recv()

        @when(l < LAYERS - 1)
        def _():
            r_copy(l + 1, piece).wait()

        def body(c):
            here = pl.ds(pl.multiple_of(w * per_row + c, CHUNK), CHUNK)
            part = pl.ds(pl.multiple_of(c, CHUNK), CHUNK)
            total = full[here].astype(F32)
            for j in range(1, half):
                total = total + came[(mine + j) % half, part].astype(F32)
            result[part] = total

        chunks(per_row, body)
        r_copy(l, piece).start()
        for k in range(half):
            p_copy(l, piece, k).wait_send()
        for j in range(1, half):
            c_copy(l, piece, (mine + j) % half, mine).wait_send()

    def v_copy(l, j, source):
        to = (w + j) % wide
        return remote(
            R["sv"].at[l], R["rv"].at[l, source],
            R["v_s"].at[l, j], R["v_r"].at[l, source], to, z,
        )

    def sm_copy(l):
        return remote(
            R["sh"].at[l, 1 - inside], R["sm"].at[l], R["sm_s"].at[l], R["sm_r"].at[l], w, mate
        )

    def v_start(l):
        @when(inner)
        def _():
            sm_copy(l).start()
            R["sv"][l, 0:8] = R["sh"][l, inside]
            sm_copy(l).wait_send()

        @when(outer)
        def _():
            sm_copy(l).wait_recv()
            R["sv"][l, 0:8] = R["sm"][l]

        for j in range(1, wide):
            v_copy(l, j, w).start()

    def v_end(l):
        total = R["sv"][l]
        for j in range(1, wide):
            source = (w + j) % wide
            v_copy(l, j, source).wait_recv()
            total = total + R["rv"][l, source]
        R["gv"][l] = total
        for j in range(1, wide):
            v_copy(l, j, w).wait_send()

    def norm_in(buf, l, branch, i):
        at_norm = 2 * l + branch
        scale = [R["gn"][j, pl.ds(G_GAIN + at_norm, 1)] for j in range(4)]
        shift = [R["gn"][j, pl.ds(G_BIAS + at_norm, 1)] for j in range(4)]
        scale = jnp.concatenate(scale, axis=1)
        shift = jnp.concatenate(shift, axis=1)

        def body(c):
            here = at(i, c)
            raw = buf[here, :].astype(F32)
            mean = jnp.sum(raw, axis=1, keepdims=True) * (1.0 / D)
            square = jnp.sum(raw * raw, axis=1, keepdims=True) * (1.0 / D)
            s = lax.rsqrt(square - mean * mean + EPS)
            R["act"][at_norm, here] = ((raw - mean) * s * scale + shift).astype(BF16)
            R["centre"][here] = R["centre"][here] + mean
            R["spread"][at_norm, here] = s

        chunks(ROWS, body, True)

    def norm_keep(l, branch, i):
        at_norm = 2 * l + branch

        @when(inner)
        def _():
            def body(c):
                here = at(i, c)
                R["n"][at_norm, here] = (R["r"][here] - R["centre"][here]) * R["spread"][
                    at_norm, here
                ]

            chunks(ROWS, body, True)

    def norm_back(bank, l, branch, i, out_row):
        at_norm = 2 * l + branch
        rs_wait(bank, i)
        t_drain(i)

        @when(inner)
        def _():
            scale = near_row(pl.ds(G_GAIN + at_norm, 1))
            t_total(i)

            def body(c, carry):
                gain_sum, bias_sum, g_sum = carry
                c = c * CHUNK
                here = at(i, c)
                part = pl.ds(pl.multiple_of(c, CHUNK), CHUNK)
                upstream = rs_sum(bank, i, part)
                normed = R["n"][at_norm, here]
                first = R["vs"][0, part, 0:1] * (1.0 / D)
                second = R["vs"][0, part, 64:65] * (1.0 / D)
                grown = R["g"][here] + (
                    upstream * scale - first - normed * second
                ) * R["spread"][at_norm, here]
                R["g"][here] = grown
                gain_sum = gain_sum + jnp.sum(upstream * normed, axis=0, keepdims=True)
                bias_sum = bias_sum + jnp.sum(upstream, axis=0, keepdims=True)
                g_sum = g_sum + jnp.sum(grown, axis=0, keepdims=True)
                return gain_sum, bias_sum, g_sum

            zero = jnp.zeros((1, 2 * width), F32)
            gain_sum, bias_sum, g_sum = lax.fori_loop(
                0, ROWS // CHUNK, body, (zero, zero, zero), unroll=True
            )
            half_add(l, V_GAIN + branch, gain_sum)
            half_add(l, V_BIAS + branch, bias_sum)
            if out_row is not None:
                half_add(l, out_row, g_sum)

    def half_add(l, row, value):
        for u in range(2):
            there = slice(row, row + 1)
            part = value[:, u * width : (u + 1) * width]
            R["sh"][l, u, there] = R["sh"][l, u, there] + part

    def send_sums(at_norm, i, block_of):
        R["vs"][0, 0:ROWS] = jnp.zeros((ROWS, 128), F32)
        R["vs"][1, 0:ROWS] = jnp.zeros((ROWS, 128), F32)
        l, branch = at_norm

        def block(j):
            y = block_of(j)
            R["tmp"][...] = y
            scale = R["gn"][j, pl.ds(G_GAIN + 2 * l + branch, 1)]
            shift = R["gn"][j, pl.ds(G_BIAS + 2 * l + branch, 1)]

            def body(c):
                part = pl.ds(pl.multiple_of(c, CHUNK), CHUNK)
                value = R["tmp"][part]
                normed = R["act"][2 * l + branch, at(i, c), cols(j)].astype(F32) - shift
                first = value * scale
                second = value * normed
                for m in range(width // 128):
                    lanes = slice(m * 128, (m + 1) * 128)
                    R["vs"][0, part] = R["vs"][0, part] + first[:, lanes]
                    R["vs"][1, part] = R["vs"][1, part] + second[:, lanes]

            chunks(ROWS, body, True)
            return R["tmp"][...]

        return block

    head_lanes = [slice(h * HEAD_DIM, (h + 1) * HEAD_DIM) for h in range(heads)]

    def attention(l, i):
        keys = pl.ds(i * KEYS, KEYS)
        column = lax.broadcasted_iota(jnp.int32, (ROWS, KEYS), 1)
        factor = 1.0 / math.sqrt(HEAD_DIM)
        scores = [
            dot_t(R["q"][l, rows(i), lanes], R["k"][l, keys, lanes]) for lanes in head_lanes
        ]
        probs = []
        for h in range(heads):
            masked = jnp.where(column < SEQ, scores[h] * factor, -jnp.inf)
            top = jnp.max(masked, axis=1, keepdims=True)
            grown = jnp.exp(masked - top)
            prob = grown / jnp.sum(grown, axis=1, keepdims=True)
            R["prob"][(l * images + i) * heads + h] = prob
            probs.append(prob.astype(BF16))
        mixed = [dot(probs[h], R["v"][l, keys, head_lanes[h]]) for h in range(heads)]
        R["o"][l, rows(i)] = jnp.concatenate(mixed, axis=1).astype(BF16)

    def f1(l, i):
        buf = R["x"].at[0]

        @when(l > 0)
        def _():
            ag_finish(buf, 0, i)

        norm_in(buf, l, 0, i)
        act = R["act"].at[2 * l, rows(i)]
        kept = pl.ds(i * KEYS, ROWS)
        bq = R["bq_in"][l, 0:1]
        bv = R["bq_in"][l, 1:2]
        R["q"][l, rows(i)] = (dot(act[...], R["wa"][l, :, 0:width]) + bq).astype(BF16)
        R["k"][l, kept] = dot(act[...], R["wa"][l, :, width : 2 * width]).astype(BF16)
        R["v"][l, kept] = (dot(act[...], R["wa"][l, :, 2 * width : 3 * width]) + bv).astype(BF16)
        attention(l, i)
        if i == 0:
            w_relay(l, 1)
            w_finish(l, 1)

        def block(j):
            return dot_t(R["o"][l, rows(i)], R["wa"][l, block_rows(j), 3 * width : 4 * width])

        rs_blocks(0, i, block)
        norm_keep(l, 0, i)

    def f2(l, i):
        buf = R["x"].at[1]
        ag_finish(buf, 1, i)
        norm_in(buf, l, 1, i)

        def body(b, _):
            lanes = cols(b)
            pre = dot(R["act"][2 * l + 1, rows(i)], R["wf"][l, :, lanes])
            pre = pre + R["bu_in"][pl.ds(l, 1), lanes]
            cdf = 0.5 * (1.0 + lax.erf(pre * 0.7071067811865476))
            R["u"][l, rows(i), lanes] = (pre * cdf).astype(BF16)
            R["slope"][l, rows(i), lanes] = (
                cdf + pre * jnp.exp(-0.5 * pre * pre) * 0.3989422804014327
            )
            return 0

        lax.fori_loop(0, hidden // width, body, 0)

        def block(j):
            return dot_t(R["u"][l, rows(i)], R["wf"][l, block_rows(j), hidden : 2 * hidden])

        rs_blocks(1, i, block)
        norm_keep(l, 1, i)

    def residual(bank, i, bias_row, kind):
        rs_wait(bank, i)

        @when(inner)
        def _():
            bias = near_row(bias_row)

            def body(c):
                here = at(i, c)
                part = pl.ds(pl.multiple_of(c, CHUNK), CHUNK)
                grown = R["r"][here] + (rs_sum(bank, i, part) + bias)
                R["r"][here] = grown
                if kind is not None:
                    out = (grown - R["centre"][here]).astype(BF16)
                    R["x"][kind, here, half_cols] = out

            chunks(ROWS, body, True)

        if kind is not None:
            ag_start(R["x"].at[kind], kind, i)

    def fin_copy(which, i):
        source = (R["r"], R["g"])[which]
        there = pl.ds(pl.multiple_of((1 - inside) * width, 128), width)
        return remote(
            source.at[rows(i), there], R["held"].at[i, which],
            R["fin_s"].at[which, i], R["fin_r"].at[which, i], w, mate,
        )

    def fin_start(which, i):
        @when(inner)
        def _():
            fin_copy(which, i).start()

    def fin_end(which, i):
        source, result = ((R["r"], R["out"]), (R["g"], R["gin"]))[which]
        there = pl.ds(i * SEQ, SEQ)

        @when(inner)
        def _():
            here = pl.ds(pl.multiple_of(inside * width, 128), width)
            result[there] = source[pl.ds(i * ROWS, SEQ), here]
            fin_copy(which, i).wait_send()

        @when(outer)
        def _():
            fin_copy(which, i).wait_recv()
            result[there] = R["held"][i, which, 0:SEQ]

    def post_f1(l, i):
        @when(l > 0)
        def _():
            ag_drain(R["x"].at[0], 0, i)

        residual(0, i, pl.ds(G_OUT + l, 1), 1)

    def post_f2(l, i, last):
        ag_drain(R["x"].at[1], 1, i)
        residual(1, i, pl.ds(G_DOWN + l, 1), None if last else 0)
        if last:
            fin_start(0, i)

    def send_grad(slot, kind, i):
        buf = R["e"].at[slot]

        @when(inner)
        def _():
            def body(c):
                here = at(i, c)
                buf[here, half_cols] = R["g"][here].astype(BF16)

            chunks(ROWS, body, True)

        ag_start(buf, kind, i)

    def b2(l, i):
        e = R["e"].at[2 * l + 1]

        @when(l < LAYERS - 1)
        def _():
            ag_finish(e, 2, i)

        def body(b, _):
            lanes = cols(b)
            back = pl.ds(pl.multiple_of(hidden + b * width, 128), width)
            dz = dot(e[rows(i), :], R["wf"][l, :, back]) * R["slope"][l, rows(i), lanes]
            R["f"][rows(i), lanes] = dz.astype(BF16)
            row = pl.ds(V_UP + b, 1)
            R["sv"][l, row] = R["sv"][l, row] + jnp.sum(dz, axis=0, keepdims=True)
            return 0

        lax.fori_loop(0, hidden // width, body, 0)

        def block(j):
            return dot_t(R["f"][rows(i)], R["wf"][l, block_rows(j), 0:hidden])

        rs_blocks(0, i, send_sums((l, 1), i, block))
        t_send(i)
        add_down(l, i)

    def b1(l, i):
        e = R["e"].at[2 * l]
        ag_finish(e, 3, i)
        keys = pl.ds(i * KEYS, KEYS)
        R["do"][...] = dot(e[rows(i), :], R["wa"][l, :, 3 * width : 4 * width]).astype(BF16)
        factor = 1.0 / math.sqrt(HEAD_DIM)
        grad_out = [R["do"][:, lanes] for lanes in head_lanes]
        dps = [dot_t(grad_out[h], R["v"][l, keys, head_lanes[h]]) for h in range(heads)]
        dvs, dss = [], []
        for h in range(heads):
            prob = R["prob"][(l * images + i) * heads + h]
            dvs.append(t_dot(prob.astype(BF16), grad_out[h])[0:ROWS])
            delta = jnp.sum(prob * dps[h], axis=1, keepdims=True)
            dss.append((prob * (dps[h] - delta) * factor).astype(BF16))
        dqs = [dot(dss[h], R["k"][l, keys, head_lanes[h]]) for h in range(heads)]
        dks = [t_dot(dss[h], R["q"][l, rows(i), head_lanes[h]])[0:ROWS] for h in range(heads)]
        dq, dk, dv = [jnp.concatenate(parts, axis=1) for parts in (dqs, dks, dvs)]
        for part, value in ((0, dq), (1, dk), (2, dv)):
            R["d"][rows(i), part * width : (part + 1) * width] = value.astype(BF16)
        for row, value in ((V_QV, dq), (V_QV + 1, dv)):
            there = slice(row, row + 1)
            R["sv"][l, there] = R["sv"][l, there] + jnp.sum(value, axis=0, keepdims=True)

        def block(j):
            return dot_t(R["d"][rows(i)], R["wa"][l, block_rows(j), 0 : 3 * width])

        rs_blocks(1, i, send_sums((l, 0), i, block))
        t_send(i)

    def add_down(l, i):
        @when(inner)
        def _():
            def body(c, total):
                return total + jnp.sum(R["g"][at(i, c * CHUNK)], axis=0, keepdims=True)

            zero = jnp.zeros((1, 2 * width), F32)
            half_add(l, V_DOWN, lax.fori_loop(0, ROWS // CHUNK, body, zero, unroll=True))

    def post_b2(l, i):
        @when(l < LAYERS - 1)
        def _():
            ag_drain(R["e"].at[2 * l + 1], 2, i)

        norm_back(0, l, 1, i, V_OUT)
        send_grad(2 * l, 3, i)

    def post_b1(l, i):
        ag_drain(R["e"].at[2 * l], 3, i)
        norm_back(1, l, 0, i, None)

        @when(l > 0)
        def _():
            send_grad(2 * l - 1, 2, i)

        @when(l == 0)
        def _():
            fin_start(1, i)

    def grad_block(b):
        block = (mine * 2 * per_row // 256 + 1 + b) % (D // 256)
        return block, pl.ds(pl.multiple_of(block * 256, 256), 256)

    def grad_ffn(l, first, last):
        def body(b, _):
            block, lanes = grad_block(b)
            up = t_dot(R["act"][2 * l + 1, :, lanes], R["f"][...])
            R["gf"][lanes, 0:hidden] = up.astype(BF16)
            down = t_dot(R["e"][2 * l + 1, :, lanes], R["u"][l])
            R["gf"][lanes, hidden : 2 * hidden] = down.astype(BF16)
            g_start(l, 1, block)
            return 0

        lax.fori_loop(first, last, body, 0)

    def grad_attention(l, first, last):
        def body(b, _):
            block, lanes = grad_block(b)
            qkv = t_dot(R["act"][2 * l, :, lanes], R["d"][...])
            R["ga"][lanes, 0 : 3 * width] = qkv.astype(BF16)
            out = t_dot(R["e"][2 * l, :, lanes], R["o"][l])
            R["ga"][lanes, 3 * width : 4 * width] = out.astype(BF16)
            g_start(l, 0, block)
            return 0

        lax.fori_loop(first, last, body, 0)

    def spread_rows(source, result):
        tokens = images * SEQ
        wide_rows = R["r"].at[:, 0:width]
        wide_rows[0:tokens] = source[...].astype(F32)
        row = lax.broadcasted_iota(jnp.int32, (ROWS, width), 0)
        for i in image:
            part = wide_rows[i * SEQ : i * SEQ + ROWS]
            result[rows(i), cols(z)] = jnp.where(row < SEQ, part, 0.0).astype(BF16)

    barrier = pltpu.get_barrier_semaphore()
    for j in range(1, wide):
        pl.semaphore_signal(barrier, 1, device_id=((w + j) % wide, z), device_id_type=MESH)
    for j in range(1, 4):
        pl.semaphore_signal(barrier, 1, device_id=(w, (z + j) % 4), device_id_type=MESH)
    image = range(images)
    first_x = R["x"].at[0]
    last_e = R["e"].at[2 * LAYERS - 1]
    R["r"][...] = jnp.zeros_like(R["r"])
    spread_rows(R["x_in"], first_x)
    for l in range(LAYERS):
        R["gb"][G_GAIN + 2 * l : G_GAIN + 2 * l + 2] = R["ng_in"][l]
        R["gb"][G_BIAS + 2 * l : G_BIAS + 2 * l + 2] = R["nb_in"][l]
    R["gb"][G_OUT : G_OUT + LAYERS] = R["bo_in"][...]
    R["gb"][G_DOWN : G_DOWN + LAYERS] = R["bd_in"][...]
    R["gn"][z] = R["gb"][...]
    for l in range(LAYERS):
        R["wo"][l] = R["wo_in"][l].T
    pl.semaphore_wait(barrier, 3 + wide - 1)

    w_start(0, 0)
    for i in image:
        a0_start(first_x, 0, i)

    def gn_copy(q, r, to):
        return remote(R["gb"], R["gn"].at[z], R["gn_s"].at[q], R["gn_r"].at[r], w, to)

    gn_copy(0, 0, mate).start()
    gn_copy(1, far, oi).start()
    gn_copy(2, far, oo).start()
    w_start(0, 1)
    for l in range(LAYERS):
        R["wd"][l] = R["wd_in"][l].T
    spread_rows(R["cot_in"], last_e)
    R["centre"][...] = jnp.zeros_like(R["centre"])
    R["sv"][...] = jnp.zeros_like(R["sv"])
    R["sh"][...] = jnp.zeros_like(R["sh"])
    R["vs"][...] = jnp.zeros_like(R["vs"])
    for name in ("k", "v"):
        for i in image:
            empty = jnp.zeros((LAYERS, KEYS - ROWS, width), BF16)
            R[name][:, i * KEYS + ROWS : (i + 1) * KEYS] = empty
    for i in image:
        a0_relay(first_x, 0, i)
    for i in image:
        a0_start(last_e, 1, i)
    w_start(0, 2)
    w_start(0, 3)
    for l in range(1, LAYERS):
        for piece in range(4):
            w_start(l, piece)
    for q in range(3):
        gn_copy(q, q, mate).wait_recv()
    for q in range(3):
        gn_copy(q, q, mate).wait_send()
    w_relay(0, 0)
    for i in image:
        a0_finish(first_x, 0, i)

    @when(inner)
    def _():
        R["r"][...] = first_x[:, half_cols].astype(F32)

    w_finish(0, 0)
    for i in image:
        a0_relay(last_e, 1, i)

    def forward(l, _):
        f1(l, 0)

        @when(l > 0)
        def _():
            ag_relay(R["x"].at[0], 0, 1)

        rs_relay(0, 0)
        f1(l, 1)
        post_f1(l, 0)
        w_relay(l, 2)
        rs_relay(0, 1)
        ag_relay(R["x"].at[1], 1, 0)
        post_f1(l, 1)
        w_finish(l, 2)
        w_relay(l, 3)
        w_finish(l, 3)

        f2(l, 0)
        ag_relay(R["x"].at[1], 1, 1)
        rs_relay(1, 0)
        f2(l, 1)

        @when(l < LAYERS - 1)
        def _():
            w_relay(l + 1, 0)
            post_f2(l, 0, False)
            rs_relay(1, 1)
            ag_relay(R["x"].at[0], 0, 0)
            post_f2(l, 1, False)
            w_finish(l + 1, 0)

        return 0

    lax.fori_loop(0, LAYERS, forward, 0)
    for i in image:
        a0_finish(last_e, 1, i)

    @when(inner)
    def _():
        R["g"][...] = last_e[:, half_cols].astype(F32)

    def backward(step, _):
        l = LAYERS - 1 - step
        top = l == LAYERS - 1
        e2 = R["e"].at[2 * l + 1]
        e1 = R["e"].at[2 * l]
        b2(l, 0)

        @when(top)
        def _():
            rs_relay(1, 1)

        @when(l < LAYERS - 1)
        def _():
            ag_relay(e2, 2, 1)

        rs_relay(0, 0)
        b2(l, 1)

        @when(top)
        def _():
            post_f2(l, 0, True)
            post_f2(l, 1, True)

        post_b2(l, 0)
        grad_ffn(l, 0, 2)
        rs_relay(0, 1)
        ag_relay(e1, 3, 0)
        post_b2(l, 1)
        grad_ffn(l, 2, 4)
        b1(l, 0)
        ag_relay(e1, 3, 1)
        rs_relay(1, 0)

        @when(l < LAYERS - 1)
        def _():
            g_end(l + 1, 0)
            v_end(l + 1)

        g_mid(l, 1)
        b1(l, 1)
        post_b1(l, 0)
        grad_attention(l, 0, 4)
        rs_relay(1, 1)

        @when(l > 0)
        def _():
            ag_relay(R["e"].at[2 * l - 1], 2, 0)

        g_mid(l, 0)
        post_b1(l, 1)
        g_end(l, 1)
        v_start(l)
        return 0

    lax.fori_loop(0, LAYERS, backward, 0)
    g_end(jnp.int32(0), 0)
    for which in range(2):
        for i in image:
            fin_end(which, i)
    v_end(0)
    for piece in range(2):
        r_copy(0, piece).wait()


def body(wide, inputs, norm_gain, norm_bias, w_qkv, b_qv, w_out, b_out, w_up, b_up, w_down, b_down, cotangent):
    tokens, width = inputs.shape
    images = tokens // SEQ
    hidden = w_up.shape[2]
    per_row = w_up.shape[1]
    half = wide // 2
    scratch = scratch_of(half, per_row, width, hidden, images)
    names = IN_NAMES + OUT_NAMES + tuple(scratch)
    vmem = pl.BlockSpec(memory_space=pltpu.VMEM)
    anywhere = pl.BlockSpec(memory_space=pl.ANY)
    out, gin, gwa, gwf, gv = pl.pallas_call(
        functools.partial(kernel, wide, images, width, hidden, names),
        out_shape=(
            jax.ShapeDtypeStruct((tokens, width), F32),
            jax.ShapeDtypeStruct((tokens, width), F32),
            jax.ShapeDtypeStruct((LAYERS, per_row, 4 * width), F32),
            jax.ShapeDtypeStruct((LAYERS, per_row, 2 * hidden), F32),
            jax.ShapeDtypeStruct((LAYERS, V_ROWS, width), F32),
        ),
        in_specs=[vmem] * 10 + [anywhere] * 2,
        out_specs=(vmem, vmem, anywhere, anywhere, vmem),
        scratch_shapes=list(scratch.values()),
        compiler_params=pltpu.CompilerParams(
            collective_id=0, has_side_effects=True, vmem_limit_bytes=67043328
        ),
        name="encoder_step",
    )(
        inputs, cotangent, norm_gain, norm_bias, b_qv, b_out, b_up, b_down, w_out, w_down,
        w_qkv.reshape(LAYERS, per_row, 3 * width), w_up,
    )
    return (
        out,
        gin,
        gv[:, V_GAIN : V_GAIN + 2],
        gv[:, V_BIAS : V_BIAS + 2],
        gwa[:, :, : 3 * width].reshape(LAYERS, per_row, 3, width),
        gv[:, V_QV : V_QV + 2],
        gwa[:, :, 3 * width :].transpose(0, 2, 1),
        gv[:, V_OUT],
        gwf[:, :, :hidden],
        gv[:, V_UP : V_UP + hidden // width].reshape(LAYERS, hidden),
        gwf[:, :, hidden:].transpose(0, 2, 1),
        gv[:, V_DOWN],
    )


def solution(mesh):
    rows = P("wide", "narrow")
    vector2 = P(None, None, "narrow")
    vector = P(None, "narrow")
    down_cols = P(None, "narrow", "wide")
    up_rows = P(None, "wide", "narrow")
    qkv = P(None, "wide", None, "narrow")
    return jax.shard_map(
        functools.partial(body, mesh.shape["wide"]),
        mesh=mesh,
        in_specs=(
            rows, vector2, vector2, qkv, vector2, down_cols, vector, up_rows, vector, down_cols,
            vector, rows,
        ),
        out_specs=(
            rows, rows, vector2, vector2, qkv, vector2, down_cols, vector, up_rows, vector,
            down_cols, vector,
        ),
        check_vma=False,
    )
```

time: 301 us -> 273 us (0.907); the launches traced: 296 us -> 273 us
  Pallas kernels: 274 us -> 257 us
  local copies, waits for them, and re-layouts: 18.1 us -> 14.6 us
    pallas_call x1, Pallas kernels: 274 us -> 257 us  [body(): pl.pallas_call(functools.partial(kernel, wide, images, width, hidden, nam...]
    reshape x7 -> x0, local copies, waits for them, and re-layouts: 6.33 us -> none  [the longest x2 2 us: padded(): shaped = matrix.reshape(images, SEQ, width)]
    unnamed x21 -> x15, local copies, waits for them, and re-layouts: 5.95 us -> 7.93 us
where the time goes in v2:
time: 273 us
  Pallas kernels  257 us (94%)
  local copies, waits for them, and re-layouts  14.6 us (5%)
    pallas_call x1, Pallas kernels, body(): pl.pallas_call(functools.partial(kernel, wide, images, width, hidden, nam...  257 us
    unnamed x15, local copies, waits for them, and re-layouts  7.93 us

profile of v2, /device:TPU:0, one launch (start us, length us, event | category | flops | bytes accessed | tf_op | source)
XLA Modules:
  0.0 272.5 jit_solution(16693821227751646785)
XLA Ops:
  0.6 1.2 copy.28
  1.9 0.9 copy.29.refs_10_
  2.8 257.2 %encoder_step.1 = (f32[394,256]{1,0:T(8,128)}, f32[394,256]{1,0:T(8,128)}, f32[2,128,1024]{2,1,0:T(8,128)}, f32[2,128,2048]{2,1,0:T(8,128)}, f32[2,16,256]{2,1,0:T(8,128)}) custom-call(bf16[394,256]{1,0:T(8,128)(2,1)} %refs_0_.1, bf16[394,256]{1,0:T(8,128)(2,1)} %refs_1_.1, f32[2,2,256]{2,1,0:T(2,128)} %refs_2_.1, f32[2,2,256]{2,1,0:T(2,128)} %refs_3_.1, ...), custom_call_target="tpu_custom_call" | custom-call | tf_op jit(solution)/shard_map/encoder_step/pallas_call | solution.py:1067
  260.0 0.8 fusion
  260.8 0.6 copy_bitcast_fusion
  261.4 0.7 slice_bitcast_fusion.2
  262.1 1.4 fusion.1
  263.5 0.6 copy.36
  264.1 1.0 slice_bitcast_fusion.1
  265.1 1.2 slice.32
  266.3 0.3 copy.30
  266.6 0.0 copy-start
  266.6 1.1 copy.31
  267.7 0.8 copy.32
  268.6 0.0 copy-done
  268.6 1.2 slice_bitcast_fusion
  269.7 0.0 copy-start.2
  269.7 0.0 copy-start.1
  269.7 1.3 copy.33
  271.0 0.0 copy-done.2
  271.0 0.8 copy.41
  271.8 0.0 copy-done.1
  271.8 0.8 copy.42
Async XLA Ops:
  266.6 2.0 copy-start
  269.7 1.3 copy-start.2
  269.7 2.1 copy-start.1

commit v3 on v2

--- a/solution.py
+++ b/solution.py
@@ -21,8 +21,9 @@
 CHUNK = 16
 HIGHEST = lax.Precision.HIGHEST
 
-V_GAIN, V_BIAS, V_OUT, V_DOWN, V_QV, V_UP = 0, 2, 4, 5, 8, 10
-V_ROWS = 16
+V_GAIN, V_BIAS, V_OUT, V_DOWN = 0, 2, 4, 5
+V_QV, V_UP = 0, 2
+V_ROWS = 8
 G_GAIN, G_BIAS, G_OUT, G_DOWN = 0, 4, 8, 10
 G_ROWS = 16
 
@@ -52,13 +53,17 @@
     dma = pltpu.SemaphoreType.DMA
     vm = pltpu.VMEM
     return dict(
-        wa=vm((LAYERS, D, 4 * width), BF16),
+        wq=vm((LAYERS, 3, D, width), BF16),
+        wp=vm((LAYERS, D, width), BF16),
         wf=vm((LAYERS, D, 2 * hidden), BF16),
-        ga=vm((D, 4 * width), BF16),
+        gq=vm((3, D, width), BF16),
+        go=vm((D, width), BF16),
         gf=vm((D, 2 * hidden), BF16),
-        pa=vm((LAYERS * half, per_row, 4 * width), BF16),
+        pq=vm((LAYERS * half, 3, per_row, width), BF16),
+        po=vm((LAYERS * half, per_row, width), BF16),
         pf=vm((half, per_row, 2 * hidden), BF16),
-        ca=vm((LAYERS * half, per_row, 4 * width), BF16),
+        cq=vm((LAYERS * half, 3, per_row, width), BF16),
+        co=vm((LAYERS * half, per_row, width), BF16),
         cf=vm((half, per_row, 2 * hidden), BF16),
         e=vm((2 * LAYERS, tall, D), BF16),
         act=vm((2 * LAYERS, tall, D), BF16),
@@ -87,12 +92,14 @@
         tr=vm((images, 3, 8, KEYS), F32),
         gb=vm((G_ROWS, width), F32),
         gn=vm((4, G_ROWS, width), F32),
-        ra=vm((per_row, 4 * width), F32),
-        rf=vm((per_row, 2 * hidden), F32),
+        rq=vm((3, per_row, width), F32),
+        ro=vm((width, per_row), F32),
+        ru=vm((per_row, hidden), F32),
+        rd=vm((hidden, per_row), F32),
         wo=vm((LAYERS, per_row, width), BF16),
         wd=vm((LAYERS, per_row, hidden), BF16),
         sh=vm((LAYERS, 2, 8, width), F32),
-        sm=vm((LAYERS, 8, width), F32),
+        rh=vm((LAYERS, 2 * half, 8, width), F32),
         sv=vm((LAYERS, V_ROWS, width), F32),
         rv=vm((LAYERS, 2 * half, V_ROWS, width), F32),
         a0_s=dma((2, images, 4)),
@@ -105,8 +112,8 @@
         t_r=dma((images, 3)),
         gn_s=dma((3,)),
         gn_r=dma((3,)),
-        sm_s=dma((LAYERS,)),
-        sm_r=dma((LAYERS,)),
+        h_s=dma((LAYERS, 2, 2 * half)),
+        h_r=dma((LAYERS, 2 * half)),
         fin_s=dma((2, images)),
         fin_r=dma((2, images)),
         w_l=dma((LAYERS, 4)),
@@ -114,11 +121,11 @@
         w_r=dma((LAYERS, 4, half)),
         w_f=dma((LAYERS, 4, half)),
         w_g=dma((LAYERS, 4, half)),
-        p_s=dma((2, half)),
-        p_r=dma((LAYERS, 2, half)),
-        c_s=dma((2, half)),
-        c_r=dma((LAYERS, 2, half)),
-        r_s=dma((LAYERS, 2)),
+        p_s=dma((3, half)),
+        p_r=dma((LAYERS, 3, half)),
+        c_s=dma((3, half)),
+        c_r=dma((LAYERS, 3, half)),
+        r_s=dma((LAYERS, 4)),
         v_s=dma((LAYERS, 2 * half)),
         v_r=dma((LAYERS, 2 * half)),
     )
@@ -128,7 +135,9 @@
     "x_in", "cot_in", "ng_in", "nb_in", "bq_in", "bo_in", "bu_in", "bd_in", "wo_in", "wd_in",
     "wq_in", "wu_in",
 )
-OUT_NAMES = ("out", "gin", "gwa", "gwf", "gv")
+OUT_NAMES = (
+    "out", "gin", "gng", "gnb", "gwq", "gbqv", "gwo", "gbo", "gwu", "gbup", "gwd", "gbd",
+)
 
 
 def kernel(wide, images, width, hidden, names, *refs):
@@ -349,33 +358,36 @@
 
     def weights(l, piece):
         if piece == 0:
-            return R["wa"].at[l, :, 0 : 3 * width], R["wq_in"].at[l]
+            return R["wq"].at[l], R["wq_in"].at[l]
         if piece == 1:
-            return R["wa"].at[l, :, 3 * width : 4 * width], R["wo"].at[l]
+            return R["wp"].at[l], R["wo"].at[l]
         if piece == 2:
             return R["wf"].at[l, :, 0:hidden], R["wu_in"].at[l]
         return R["wf"].at[l, :, hidden : 2 * hidden], R["wd"].at[l]
 
+    def rows_of(ref, k):
+        return ref.at[wrows(k)] if len(ref.shape) == 2 else ref.at[:, wrows(k)]
+
     def w_local(l, piece):
         full, shard = weights(l, piece)
-        return pltpu.make_async_copy(shard, full.at[wrows(w)], R["w_l"].at[l, piece])
+        return pltpu.make_async_copy(shard, rows_of(full, w), R["w_l"].at[l, piece])
 
     def w_send(l, piece, s, to):
         full, shard = weights(l, piece)
         return remote(
-            shard, full.at[wrows(w)], R["w_s"].at[l, piece, s], R["w_r"].at[l, piece, mine], to, z
+            shard, rows_of(full, w), R["w_s"].at[l, piece, s], R["w_r"].at[l, piece, mine], to, z
         )
 
     def w_pair(l, piece):
         full, shard = weights(l, piece)
         return remote(
-            shard, full.at[wrows(w)],
+            shard, rows_of(full, w),
             R["w_s"].at[l, piece, half - 1], R["w_f"].at[l, piece, mine], partner, z,
         )
 
     def w_cross(l, piece, k, parity):
         full, _ = weights(l, piece)
-        part = full.at[wrows(2 * k + parity)]
+        part = rows_of(full, 2 * k + parity)
         return remote(
             part, part, R["w_g"].at[l, piece, k], R["w_f"].at[l, piece, k], partner, z
         )
@@ -391,7 +403,7 @@
         for j in range(1, half):
             k = (mine + half - j) % half
             remote(
-                shard, full.at[wrows(2 * k + par)],
+                shard, rows_of(full, 2 * k + par),
                 R["w_s"].at[l, piece, 0], R["w_r"].at[l, piece, k], partner, z,
             ).wait_recv()
             w_cross(l, piece, k, par).start()
@@ -407,28 +419,37 @@
             w_cross(l, piece, (mine + j) % half, par).wait_send()
 
     def grads(l, piece):
+        if piece == 1:
+            return R["gf"], R["pf"], R["cf"]
+        room = pl.ds(l * half, half)
         if piece == 0:
-            room = pl.ds(l * half, half)
-            return R["ga"], R["pa"].at[room], R["ca"].at[room], R["ra"], R["gwa"].at[l]
-        return R["gf"], R["pf"], R["cf"], R["rf"], R["gwf"].at[l]
+            return R["gq"], R["pq"].at[room], R["cq"].at[room]
+        return R["go"], R["po"].at[room], R["co"].at[room]
 
     def p_copy(l, piece, k):
-        full, theirs, _, _, _ = grads(l, piece)
+        full, theirs, _ = grads(l, piece)
         return remote(
-            full.at[wrows(2 * k + 1 - par)], theirs.at[k],
+            rows_of(full, 2 * k + 1 - par), theirs.at[k],
             R["p_s"].at[piece, k], R["p_r"].at[l, piece, k], partner, z,
         )
 
     def c_copy(l, piece, k, source):
-        full, _, came, _, _ = grads(l, piece)
+        full, _, came = grads(l, piece)
         return remote(
-            full.at[wrows(2 * k + par)], came.at[source],
+            rows_of(full, 2 * k + par), came.at[source],
             R["c_s"].at[piece, k], R["c_r"].at[l, piece, source], 2 * k + par, z,
         )
 
-    def r_copy(l, piece):
-        _, _, _, total, result = grads(l, piece)
-        return pltpu.make_async_copy(total, result, R["r_s"].at[l, piece])
+    def r_copies(l, piece):
+        pairs = (
+            ((R["rq"], R["gwq"]),),
+            ((R["ru"], R["gwu"]), (R["rd"], R["gwd"])),
+            ((R["ro"], R["gwo"]),),
+        )[piece]
+        return [
+            pltpu.make_async_copy(total, result.at[l], R["r_s"].at[l, piece + 2 * q])
+            for q, (total, result) in enumerate(pairs)
+        ]
 
     def g_start(l, piece, b):
         pairs = half * 256 // D
@@ -436,42 +457,61 @@
             p_copy(l, piece, b * pairs + k).start()
 
     def g_mid(l, piece):
-        full, theirs, _, _, _ = grads(l, piece)
+        full, theirs, _ = grads(l, piece)
         for j in range(1, half + 1):
             k = (mine + j) % half
             p_copy(l, piece, k).wait_recv()
 
             def body(c):
                 here = pl.ds(pl.multiple_of((2 * k + par) * per_row + c, CHUNK), CHUNK)
-                total = full[here].astype(F32) + theirs[
-                    k, pl.ds(pl.multiple_of(c, CHUNK), CHUNK)
-                ].astype(F32)
-                full[here] = total.astype(BF16)
+                part = pl.ds(pl.multiple_of(c, CHUNK), CHUNK)
+                ours = full.at[:, here] if piece == 0 else full.at[here]
+                other = theirs.at[k, :, part] if piece == 0 else theirs.at[k, part]
+                ours[...] = (ours[...].astype(F32) + other[...].astype(F32)).astype(BF16)
 
             chunks(per_row, body)
             if j < half:
                 c_copy(l, piece, k, mine).start()
 
     def g_end(l, piece):
-        full, _, came, result, _ = grads(l, piece)
+        full, _, came = grads(l, piece)
         for j in range(1, half):
             k = (mine + half - j) % half
             c_copy(l, piece, k, k).wait_recv()
 
         @when(l < LAYERS - 1)
         def _():
-            r_copy(l + 1, piece).wait()
-
-        def body(c):
-            here = pl.ds(pl.multiple_of(w * per_row + c, CHUNK), CHUNK)
-            part = pl.ds(pl.multiple_of(c, CHUNK), CHUNK)
-            total = full[here].astype(F32)
-            for j in range(1, half):
-                total = total + came[(mine + j) % half, part].astype(F32)
-            result[part] = total
-
-        chunks(per_row, body)
-        r_copy(l, piece).start()
+            for copy in r_copies(l + 1, piece):
+                copy.wait()
+
+        others = [(mine + j) % half for j in range(1, half)]
+        if piece != 2:
+            def body(c):
+                part = pl.ds(pl.multiple_of(c, CHUNK), CHUNK)
+                here = pl.ds(pl.multiple_of(w * per_row + c, CHUNK), CHUNK)
+                if piece == 0:
+                    total = full[:, here].astype(F32)
+                    for k in others:
+                        total = total + came[k, :, part].astype(F32)
+                    R["rq"][:, part] = total
+                else:
+                    total = full[here, 0:hidden].astype(F32)
+                    for k in others:
+                        total = total + came[k, part, 0:hidden].astype(F32)
+                    R["ru"][part] = total
+
+            chunks(per_row, body)
+        if piece != 0:
+            first = hidden if piece == 1 else 0
+            result = R["rd"] if piece == 1 else R["ro"]
+            for c in range(0, result.shape[0], 256):
+                lanes = slice(first + c, first + c + 256)
+                total = full[wrows(w), lanes].astype(F32)
+                for k in others:
+                    total = total + came[k, :, lanes].astype(F32)
+                result[c : c + 256] = total.T
+        for copy in r_copies(l, piece):
+            copy.start()
         for k in range(half):
             p_copy(l, piece, k).wait_send()
         for j in range(1, half):
@@ -484,25 +524,26 @@
             R["v_s"].at[l, j], R["v_r"].at[l, source], to, z,
         )
 
-    def sm_copy(l):
+    def h_copy(l, j, source, to_mate):
+        to = (w + j) % wide
+        block, narrow = (1 - inside, mate) if to_mate else (inside, z)
         return remote(
-            R["sh"].at[l, 1 - inside], R["sm"].at[l], R["sm_s"].at[l], R["sm_r"].at[l], w, mate
+            R["sh"].at[l, block], R["rh"].at[l, source],
+            R["h_s"].at[l, 1 if to_mate else 0, j], R["h_r"].at[l, source], to, narrow,
         )
 
     def v_start(l):
-        @when(inner)
-        def _():
-            sm_copy(l).start()
-            R["sv"][l, 0:8] = R["sh"][l, inside]
-            sm_copy(l).wait_send()
-
-        @when(outer)
-        def _():
-            sm_copy(l).wait_recv()
-            R["sv"][l, 0:8] = R["sm"][l]
-
         for j in range(1, wide):
             v_copy(l, j, w).start()
+
+    def h_start(l):
+        @when(inner)
+        def _():
+            for j in range(wide):
+                if j > 0:
+                    h_copy(l, j, w, False).start()
+                h_copy(l, j, w, True).start()
+            R["rh"][l, w] = R["sh"][l, inside]
 
     def v_end(l):
         total = R["sv"][l]
@@ -510,9 +551,33 @@
             source = (w + j) % wide
             v_copy(l, j, source).wait_recv()
             total = total + R["rv"][l, source]
-        R["gv"][l] = total
+        R["gbqv"][l] = total[0:2]
+        for b in range(hidden // width):
+            R["gbup"][pl.ds(l, 1), b * width : (b + 1) * width] = total[2 + b : 3 + b]
         for j in range(1, wide):
             v_copy(l, j, w).wait_send()
+
+    def h_end(l):
+        @when(outer)
+        def _():
+            h_copy(l, 0, w, True).wait_recv()
+
+        total = R["rh"][l, w]
+        for j in range(1, wide):
+            source = (w + j) % wide
+            h_copy(l, j, source, True).wait_recv()
+            total = total + R["rh"][l, source]
+        R["gng"][l] = total[V_GAIN : V_GAIN + 2]
+        R["gnb"][l] = total[V_BIAS : V_BIAS + 2]
+        R["gbo"][pl.ds(l, 1)] = total[V_OUT : V_OUT + 1]
+        R["gbd"][pl.ds(l, 1)] = total[V_DOWN : V_DOWN + 1]
+
+        @when(inner)
+        def _():
+            for j in range(wide):
+                if j > 0:
+                    h_copy(l, j, w, False).wait_send()
+                h_copy(l, j, w, True).wait_send()
 
     def norm_in(buf, l, branch, i):
         at_norm = 2 * l + branch
@@ -648,16 +713,20 @@
         kept = pl.ds(i * KEYS, ROWS)
         bq = R["bq_in"][l, 0:1]
         bv = R["bq_in"][l, 1:2]
-        R["q"][l, rows(i)] = (dot(act[...], R["wa"][l, :, 0:width]) + bq).astype(BF16)
-        R["k"][l, kept] = dot(act[...], R["wa"][l, :, width : 2 * width]).astype(BF16)
-        R["v"][l, kept] = (dot(act[...], R["wa"][l, :, 2 * width : 3 * width]) + bv).astype(BF16)
+        R["q"][l, rows(i)] = (dot(act[...], R["wq"][l, 0]) + bq).astype(BF16)
+        R["k"][l, kept] = dot(act[...], R["wq"][l, 1]).astype(BF16)
+        R["v"][l, kept] = (dot(act[...], R["wq"][l, 2]) + bv).astype(BF16)
+        if i == 0:
+            @when(l == 0)
+            def _():
+                w_relay(l, 1)
+
         attention(l, i)
         if i == 0:
-            w_relay(l, 1)
             w_finish(l, 1)
 
         def block(j):
-            return dot_t(R["o"][l, rows(i)], R["wa"][l, block_rows(j), 3 * width : 4 * width])
+            return dot_t(R["o"][l, rows(i)], R["wp"][l, block_rows(j)])
 
         rs_blocks(0, i, block)
         norm_keep(l, 0, i)
@@ -679,6 +748,8 @@
             return 0
 
         lax.fori_loop(0, hidden // width, body, 0)
+        if i == 0:
+            w_finish(l, 3)
 
         def block(j):
             return dot_t(R["u"][l, rows(i)], R["wf"][l, block_rows(j), hidden : 2 * hidden])
@@ -790,14 +861,16 @@
         e = R["e"].at[2 * l]
         ag_finish(e, 3, i)
         keys = pl.ds(i * KEYS, KEYS)
-        R["do"][...] = dot(e[rows(i), :], R["wa"][l, :, 3 * width : 4 * width]).astype(BF16)
+        R["do"][...] = dot(e[rows(i), :], R["wp"][l]).astype(BF16)
+        if i == images - 1:
+            grad_out(l)
         factor = 1.0 / math.sqrt(HEAD_DIM)
-        grad_out = [R["do"][:, lanes] for lanes in head_lanes]
-        dps = [dot_t(grad_out[h], R["v"][l, keys, head_lanes[h]]) for h in range(heads)]
+        dos = [R["do"][:, lanes] for lanes in head_lanes]
+        dps = [dot_t(dos[h], R["v"][l, keys, head_lanes[h]]) for h in range(heads)]
         dvs, dss = [], []
         for h in range(heads):
             prob = R["prob"][(l * images + i) * heads + h]
-            dvs.append(t_dot(prob.astype(BF16), grad_out[h])[0:ROWS])
+            dvs.append(t_dot(prob.astype(BF16), dos[h])[0:ROWS])
             delta = jnp.sum(prob * dps[h], axis=1, keepdims=True)
             dss.append((prob * (dps[h] - delta) * factor).astype(BF16))
         dqs = [dot(dss[h], R["k"][l, keys, head_lanes[h]]) for h in range(heads)]
@@ -810,7 +883,11 @@
             R["sv"][l, there] = R["sv"][l, there] + jnp.sum(value, axis=0, keepdims=True)
 
         def block(j):
-            return dot_t(R["d"][rows(i)], R["wa"][l, block_rows(j), 0 : 3 * width])
+            parts = [
+                dot_t(R["d"][rows(i), m * width : (m + 1) * width], R["wq"][l, m, block_rows(j)])
+                for m in range(3)
+            ]
+            return parts[0] + parts[1] + parts[2]
 
         rs_blocks(1, i, send_sums((l, 0), i, block))
         t_send(i)
@@ -860,17 +937,26 @@
 
         lax.fori_loop(first, last, body, 0)
 
-    def grad_attention(l, first, last):
+    def grad_qkv(l):
         def body(b, _):
             block, lanes = grad_block(b)
             qkv = t_dot(R["act"][2 * l, :, lanes], R["d"][...])
-            R["ga"][lanes, 0 : 3 * width] = qkv.astype(BF16)
-            out = t_dot(R["e"][2 * l, :, lanes], R["o"][l])
-            R["ga"][lanes, 3 * width : 4 * width] = out.astype(BF16)
+            for m in range(3):
+                R["gq"][m, lanes] = qkv[:, m * width : (m + 1) * width].astype(BF16)
             g_start(l, 0, block)
             return 0
 
-        lax.fori_loop(first, last, body, 0)
+        lax.fori_loop(0, D // 256, body, 0)
+
+    def grad_out(l):
+        def body(b, _):
+            block, lanes = grad_block(b)
+            out = t_dot(R["e"][2 * l, :, lanes], R["o"][l])
+            R["go"][lanes] = out.astype(BF16)
+            g_start(l, 2, block)
+            return 0
+
+        lax.fori_loop(0, D // 256, body, 0)
 
     def spread_rows(source, result):
         tokens = images * SEQ
@@ -961,11 +1047,9 @@
         w_relay(l, 2)
         rs_relay(0, 1)
         ag_relay(R["x"].at[1], 1, 0)
+        w_relay(l, 3)
         post_f1(l, 1)
         w_finish(l, 2)
-        w_relay(l, 3)
-        w_finish(l, 3)
-
         f2(l, 0)
         ag_relay(R["x"].at[1], 1, 1)
         rs_relay(1, 0)
@@ -977,6 +1061,7 @@
             post_f2(l, 0, False)
             rs_relay(1, 1)
             ag_relay(R["x"].at[0], 0, 0)
+            w_relay(l + 1, 1)
             post_f2(l, 1, False)
             w_finish(l + 1, 0)
 
@@ -1013,45 +1098,74 @@
             post_f2(l, 0, True)
             post_f2(l, 1, True)
 
+        grad_ffn(l, 0, 2)
         post_b2(l, 0)
-        grad_ffn(l, 0, 2)
+        grad_ffn(l, 2, 4)
         rs_relay(0, 1)
+
+        @when(l < LAYERS - 1)
+        def _():
+            g_end(l + 1, 0)
+            g_end(l + 1, 2)
+            v_end(l + 1)
+            h_end(l + 1)
+
+        g_mid(l, 1)
         ag_relay(e1, 3, 0)
         post_b2(l, 1)
-        grad_ffn(l, 2, 4)
         b1(l, 0)
         ag_relay(e1, 3, 1)
         rs_relay(1, 0)
 
-        @when(l < LAYERS - 1)
-        def _():
-            g_end(l + 1, 0)
-            v_end(l + 1)
-
-        g_mid(l, 1)
         b1(l, 1)
         post_b1(l, 0)
-        grad_attention(l, 0, 4)
+        grad_qkv(l)
+        g_mid(l, 2)
+        g_mid(l, 0)
         rs_relay(1, 1)
 
         @when(l > 0)
         def _():
             ag_relay(R["e"].at[2 * l - 1], 2, 0)
 
-        g_mid(l, 0)
-        post_b1(l, 1)
         g_end(l, 1)
         v_start(l)
+        post_b1(l, 1)
+        h_start(l)
         return 0
 
     lax.fori_loop(0, LAYERS, backward, 0)
-    g_end(jnp.int32(0), 0)
-    for which in range(2):
-        for i in image:
-            fin_end(which, i)
+    first = jnp.int32(0)
+    g_end(first, 2)
     v_end(0)
-    for piece in range(2):
-        r_copy(0, piece).wait()
+    for i in image:
+        fin_end(0, i)
+    g_end(first, 0)
+    for i in image:
+        fin_end(1, i)
+    h_end(0)
+    for piece in range(3):
+        for copy in r_copies(0, piece):
+            copy.wait()
+
+
+def deliver(*refs):
+    count = (len(refs) - 2) // 3
+    sources, results, rooms = (refs[i * count : (i + 1) * count] for i in range(3))
+    came, gone = refs[3 * count :]
+
+    def copy(i, inward):
+        if inward:
+            return pltpu.make_async_copy(sources[i], rooms[i], came.at[i])
+        return pltpu.make_async_copy(rooms[i], results[i], gone.at[i])
+
+    for i in range(count):
+        copy(i, True).start()
+    for i in range(count):
+        copy(i, True).wait()
+        copy(i, False).start()
+    for i in range(count):
+        copy(i, False).wait()
 
 
 def body(wide, inputs, norm_gain, norm_bias, w_qkv, b_qv, w_out, b_out, w_up, b_up, w_down, b_down, cotangent):
@@ -1064,17 +1178,30 @@
     names = IN_NAMES + OUT_NAMES + tuple(scratch)
     vmem = pl.BlockSpec(memory_space=pltpu.VMEM)
     anywhere = pl.BlockSpec(memory_space=pl.ANY)
-    out, gin, gwa, gwf, gv = pl.pallas_call(
+
+    def shaped(*shape):
+        return jax.ShapeDtypeStruct(shape, F32)
+
+    results = pl.pallas_call(
         functools.partial(kernel, wide, images, width, hidden, names),
         out_shape=(
-            jax.ShapeDtypeStruct((tokens, width), F32),
-            jax.ShapeDtypeStruct((tokens, width), F32),
-            jax.ShapeDtypeStruct((LAYERS, per_row, 4 * width), F32),
-            jax.ShapeDtypeStruct((LAYERS, per_row, 2 * hidden), F32),
-            jax.ShapeDtypeStruct((LAYERS, V_ROWS, width), F32),
+            shaped(tokens, width),
+            shaped(tokens, width),
+            shaped(LAYERS, 2, width),
+            shaped(LAYERS, 2, width),
+            shaped(LAYERS, 3, per_row, width),
+            shaped(LAYERS, 2, width),
+            shaped(LAYERS, width, per_row),
+            shaped(LAYERS, width),
+            shaped(LAYERS, per_row, hidden),
+            shaped(LAYERS, hidden),
+            shaped(LAYERS, hidden, per_row),
+            shaped(LAYERS, width),
         ),
         in_specs=[vmem] * 10 + [anywhere] * 2,
-        out_specs=(vmem, vmem, anywhere, anywhere, vmem),
+        out_specs=(
+            vmem, vmem, vmem, vmem, anywhere, vmem, anywhere, vmem, anywhere, vmem, anywhere, vmem,
+        ),
         scratch_shapes=list(scratch.values()),
         compiler_params=pltpu.CompilerParams(
             collective_id=0, has_side_effects=True, vmem_limit_bytes=67043328
@@ -1082,22 +1209,21 @@
         name="encoder_step",
     )(
         inputs, cotangent, norm_gain, norm_bias, b_qv, b_out, b_up, b_down, w_out, w_down,
-        w_qkv.reshape(LAYERS, per_row, 3 * width), w_up,
+        w_qkv.transpose(0, 2, 1, 3), w_up,
     )
-    return (
-        out,
-        gin,
-        gv[:, V_GAIN : V_GAIN + 2],
-        gv[:, V_BIAS : V_BIAS + 2],
-        gwa[:, :, : 3 * width].reshape(LAYERS, per_row, 3, width),
-        gv[:, V_QV : V_QV + 2],
-        gwa[:, :, 3 * width :].transpose(0, 2, 1),
-        gv[:, V_OUT],
-        gwf[:, :, :hidden],
-        gv[:, V_UP : V_UP + hidden // width].reshape(LAYERS, hidden),
-        gwf[:, :, hidden:].transpose(0, 2, 1),
-        gv[:, V_DOWN],
-    )
+    shapes = [result.shape for result in results]
+    count = len(shapes)
+    done = pl.pallas_call(
+        deliver,
+        out_shape=[shaped(*shape) for shape in shapes],
+        in_specs=[anywhere] * count,
+        out_specs=[anywhere] * count,
+        scratch_shapes=[pltpu.VMEM(shape, F32) for shape in shapes]
+        + [pltpu.SemaphoreType.DMA((count,))] * 2,
+        compiler_params=pltpu.CompilerParams(vmem_limit_bytes=67043328),
+        name="deliver",
+    )(*results)
+    return (*done[:4], done[4].transpose(0, 2, 1, 3), *done[5:])
 
 
 def solution(mesh):

time: 273 us -> 237 us (0.87)
  Pallas kernels: 257 us -> 236 us
  local copies, waits for them, and re-layouts: 14.6 us -> 0 us
    pallas_call x1, Pallas kernels: 257 us -> 232 us  [body(): pl.pallas_call(functools.partial(kernel, wide, images, width, hidden, nam...]
    unnamed x15 -> x0, local copies, waits for them, and re-layouts: 7.93 us -> none
    pallas_call x0 -> x1, Pallas kernels: none -> 3.82 us  [body(): pl.pallas_call(deliver, out_shape=[shaped(*shape) for shape in shapes], i...]
    slice x4 -> x0, local copies, waits for them, and re-layouts: 3.64 us -> none  [the longest x2 1.44 us: body(): gwa[:, :, :3 * width].reshape(LAYERS, per_row, 3, width)]
where the time goes in v3:
time: 237 us
  Pallas kernels  236 us (100%)
    pallas_call x1, Pallas kernels, body(): pl.pallas_call(functools.partial(kernel, wide, images, width, hidden, nam...  232 us

profile of v3, /device:TPU:0, one launch (start us, length us, event | category | flops | bytes accessed | tf_op | source)
XLA Modules:
  0.0 236.8 jit_solution(17630132528102251074)
XLA Ops:
  0.6 232.2 %encoder_step.1 = (f32[394,256]{1,0:T(8,128)}, f32[394,256]{1,0:T(8,128)}, f32[2,2,256]{2,1,0:T(2,128)}, f32[2,2,256]{2,1,0:T(2,128)}, f32[2,3,128,256]{3,2,1,0:...) custom-call(bf16[394,256]{1,0:T(8,128)(2,1)} %refs_0_.1, ...), custom_call_target="tpu_custom_call" | custom-call | tf_op jit(solution)/shard_map/encoder_step/pallas_call | solution.py:1185
  232.8 3.8 %deliver.1 = (f32[394,256]{1,0:T(8,128)}, f32[394,256]{1,0:T(8,128)}, f32[2,2,256]{2,1,0:T(2,128)}, f32[2,2,256]{2,1,0:T(2,128)}, f32[2,3,128,256]{3,2,1,0:T(8,1...) custom-call(f32[394,256]{1,0:T(8,128)} %get-tuple-element.36.refs_0_, ...), custom_call_target="tpu_custom_call" | custom-call | tf_op jit(solution)/shard_map/deliver/pallas_call | solution.py:1216

commit v4 on v3

--- a/solution.py
+++ b/solution.py
@@ -195,8 +195,8 @@
         return remote(part, part, R["a0_s"].at[kind, i, s], R["a0_r"].at[kind, i, r], w, to)
 
     def a0_start(buf, kind, i):
+        a0_copy(buf, kind, i, z, 1, far, oi).start()
         a0_copy(buf, kind, i, z, 0, 0, mate).start()
-        a0_copy(buf, kind, i, z, 1, far, oi).start()
 
     def a0_relay(buf, kind, i):
         @when(inner)
@@ -225,13 +225,9 @@
         part = buf.at[rows(i), cols(block)]
         return remote(part, part, R["ag_s"].at[kind, i, s], R["ag_r"].at[kind, i, r], w, to)
 
-    def ag_start(buf, kind, i):
-        @when(inner)
-        def _():
-            for u in range(2):
-                ag_copy(buf, kind, i, near_half + u, u, u, oi).start()
-            for u in range(2):
-                ag_copy(buf, kind, i, near_half + u, 2 + u, 2 + u, mate).start()
+    def ag_unit(buf, kind, i, u):
+        ag_copy(buf, kind, i, near_half + u, u, u, oi).start()
+        ag_copy(buf, kind, i, near_half + u, 2 + u, 2 + u, mate).start()
 
     def ag_relay(buf, kind, i):
         @when(inner)
@@ -292,13 +288,13 @@
                 chunks(ROWS, body, True)
                 rs_copy(bank, i, q, 4 + q, oi).start()
 
-    def rs_wait(bank, i):
-        @when(inner)
-        def _():
-            for q in range(2, 4):
-                rs_copy(bank, i, q, q, mate).wait_recv()
-            for q in range(2):
-                rs_copy(bank, i, q, 4 + q, oi).wait_recv()
+    def rs_unit(bank, i, u):
+        rs_copy(bank, i, 2 + u, 2 + u, mate).wait_recv()
+        rs_copy(bank, i, u, 4 + u, oi).wait_recv()
+
+    def rs_drain(bank, i):
+        @when(inner)
+        def _():
             for q in range(2):
                 rs_copy(bank, i, q, 4 + q, oi).wait_send()
 
@@ -307,20 +303,13 @@
             for q in range(4):
                 rs_copy(bank, i, q, q, mate).wait_send()
 
-    def rs_sum(bank, i, part):
+    def rs_sum(bank, i, u, part):
         slots = R["slot"]
-        return jnp.concatenate(
-            [
-                R["own"][bank, i, u, part]
-                + slots[bank, i, 2 + u, part].astype(F32)
-                + slots[bank, i, 4 + u, part].astype(F32)
-                for u in range(2)
-            ],
-            axis=1,
-        )
-
-    def near_row(row):
-        return jnp.concatenate([R["gn"][near_half + u, row] for u in range(2)], axis=1)
+        return (
+            R["own"][bank, i, u, part]
+            + slots[bank, i, 2 + u, part].astype(F32)
+            + slots[bank, i, 4 + u, part].astype(F32)
+        )
 
     def t_copy(i, q, r, to):
         return remote(
@@ -611,48 +600,66 @@
 
             chunks(ROWS, body, True)
 
-    def norm_back(bank, l, branch, i, out_row):
+    def norm_back(bank, l, branch, i, buf, kind):
         at_norm = 2 * l + branch
-        rs_wait(bank, i)
+
+        @when(inner)
+        def _():
+            t_total(i)
+            for u in range(2):
+                lanes = slice(u * width, (u + 1) * width)
+                scale = R["gn"][near_half + u, pl.ds(G_GAIN + at_norm, 1)]
+                rs_unit(bank, i, u)
+
+                def body(c):
+                    here = at(i, c)
+                    part = pl.ds(pl.multiple_of(c, CHUNK), CHUNK)
+                    upstream = rs_sum(bank, i, u, part)
+                    R["own"][bank, i, u, part] = upstream
+                    first = R["vs"][0, part, 0:1] * (1.0 / D)
+                    second = R["vs"][0, part, 64:65] * (1.0 / D)
+                    normed = R["n"][at_norm, here, lanes]
+                    grown = R["g"][here, lanes] + (
+                        upstream * scale - first - normed * second
+                    ) * R["spread"][at_norm, here]
+                    R["g"][here, lanes] = grown
+                    if buf is not None:
+                        buf[here, cols(near_half + u)] = grown.astype(BF16)
+
+                chunks(ROWS, body, True)
+                if buf is not None:
+                    ag_unit(buf, kind, i, u)
+
+    def norm_sums(bank, l, branch, i, out_row):
+        rs_drain(bank, i)
         t_drain(i)
 
         @when(inner)
         def _():
-            scale = near_row(pl.ds(G_GAIN + at_norm, 1))
-            t_total(i)
-
-            def body(c, carry):
-                gain_sum, bias_sum, g_sum = carry
-                c = c * CHUNK
-                here = at(i, c)
-                part = pl.ds(pl.multiple_of(c, CHUNK), CHUNK)
-                upstream = rs_sum(bank, i, part)
-                normed = R["n"][at_norm, here]
-                first = R["vs"][0, part, 0:1] * (1.0 / D)
-                second = R["vs"][0, part, 64:65] * (1.0 / D)
-                grown = R["g"][here] + (
-                    upstream * scale - first - normed * second
-                ) * R["spread"][at_norm, here]
-                R["g"][here] = grown
-                gain_sum = gain_sum + jnp.sum(upstream * normed, axis=0, keepdims=True)
-                bias_sum = bias_sum + jnp.sum(upstream, axis=0, keepdims=True)
-                g_sum = g_sum + jnp.sum(grown, axis=0, keepdims=True)
-                return gain_sum, bias_sum, g_sum
-
-            zero = jnp.zeros((1, 2 * width), F32)
-            gain_sum, bias_sum, g_sum = lax.fori_loop(
-                0, ROWS // CHUNK, body, (zero, zero, zero), unroll=True
-            )
-            half_add(l, V_GAIN + branch, gain_sum)
-            half_add(l, V_BIAS + branch, bias_sum)
-            if out_row is not None:
-                half_add(l, out_row, g_sum)
-
-    def half_add(l, row, value):
-        for u in range(2):
-            there = slice(row, row + 1)
-            part = value[:, u * width : (u + 1) * width]
-            R["sh"][l, u, there] = R["sh"][l, u, there] + part
+            for u in range(2):
+                lanes = slice(u * width, (u + 1) * width)
+
+                def body(c, carry):
+                    c = c * CHUNK
+                    here = at(i, c)
+                    upstream = R["own"][bank, i, u, pl.ds(pl.multiple_of(c, CHUNK), CHUNK)]
+                    normed = R["n"][2 * l + branch, here, lanes]
+                    values = (upstream * normed, upstream, R["g"][here, lanes])
+                    return tuple(
+                        total + jnp.sum(value, axis=0, keepdims=True)
+                        for total, value in zip(carry, values)
+                    )
+
+                zero = jnp.zeros((1, width), F32)
+                sums = lax.fori_loop(0, ROWS // CHUNK, body, (zero,) * 3, unroll=True)
+                small_add(l, u, V_GAIN + branch, sums[0])
+                small_add(l, u, V_BIAS + branch, sums[1])
+                if out_row is not None:
+                    small_add(l, u, out_row, sums[2])
+
+    def small_add(l, u, row, value):
+        there = slice(row, row + 1)
+        R["sh"][l, u, there] = R["sh"][l, u, there] + value
 
     def send_sums(at_norm, i, block_of):
         R["vs"][0, 0:ROWS] = jnp.zeros((ROWS, 128), F32)
@@ -681,21 +688,21 @@
 
         return block
 
+    factor = 1.0 / math.sqrt(HEAD_DIM)
     head_lanes = [slice(h * HEAD_DIM, (h + 1) * HEAD_DIM) for h in range(heads)]
 
     def attention(l, i):
         keys = pl.ds(i * KEYS, KEYS)
         column = lax.broadcasted_iota(jnp.int32, (ROWS, KEYS), 1)
-        factor = 1.0 / math.sqrt(HEAD_DIM)
         scores = [
             dot_t(R["q"][l, rows(i), lanes], R["k"][l, keys, lanes]) for lanes in head_lanes
         ]
         probs = []
         for h in range(heads):
-            masked = jnp.where(column < SEQ, scores[h] * factor, -jnp.inf)
+            masked = jnp.where(column < SEQ, scores[h], -jnp.inf)
             top = jnp.max(masked, axis=1, keepdims=True)
             grown = jnp.exp(masked - top)
-            prob = grown / jnp.sum(grown, axis=1, keepdims=True)
+            prob = grown * (1.0 / jnp.sum(grown, axis=1, keepdims=True))
             R["prob"][(l * images + i) * heads + h] = prob
             probs.append(prob.astype(BF16))
         mixed = [dot(probs[h], R["v"][l, keys, head_lanes[h]]) for h in range(heads)]
@@ -713,7 +720,8 @@
         kept = pl.ds(i * KEYS, ROWS)
         bq = R["bq_in"][l, 0:1]
         bv = R["bq_in"][l, 1:2]
-        R["q"][l, rows(i)] = (dot(act[...], R["wq"][l, 0]) + bq).astype(BF16)
+        queries = (dot(act[...], R["wq"][l, 0]) + bq).astype(BF16).astype(F32) * factor
+        R["q"][l, rows(i)] = queries.astype(BF16)
         R["k"][l, kept] = dot(act[...], R["wq"][l, 1]).astype(BF16)
         R["v"][l, kept] = (dot(act[...], R["wq"][l, 2]) + bv).astype(BF16)
         if i == 0:
@@ -747,7 +755,7 @@
             )
             return 0
 
-        lax.fori_loop(0, hidden // width, body, 0)
+        lax.fori_loop(0, hidden // width, body, 0, unroll=True)
         if i == 0:
             w_finish(l, 3)
 
@@ -758,25 +766,27 @@
         norm_keep(l, 1, i)
 
     def residual(bank, i, bias_row, kind):
-        rs_wait(bank, i)
-
-        @when(inner)
-        def _():
-            bias = near_row(bias_row)
-
-            def body(c):
-                here = at(i, c)
-                part = pl.ds(pl.multiple_of(c, CHUNK), CHUNK)
-                grown = R["r"][here] + (rs_sum(bank, i, part) + bias)
-                R["r"][here] = grown
+        @when(inner)
+        def _():
+            for u in range(2):
+                lanes = slice(u * width, (u + 1) * width)
+                bias = R["gn"][near_half + u, bias_row]
+                rs_unit(bank, i, u)
+
+                def body(c):
+                    here = at(i, c)
+                    part = pl.ds(pl.multiple_of(c, CHUNK), CHUNK)
+                    grown = R["r"][here, lanes] + (rs_sum(bank, i, u, part) + bias)
+                    R["r"][here, lanes] = grown
+                    if kind is not None:
+                        out = (grown - R["centre"][here]).astype(BF16)
+                        R["x"][kind, here, cols(near_half + u)] = out
+
+                chunks(ROWS, body, True)
                 if kind is not None:
-                    out = (grown - R["centre"][here]).astype(BF16)
-                    R["x"][kind, here, half_cols] = out
-
-            chunks(ROWS, body, True)
-
-        if kind is not None:
-            ag_start(R["x"].at[kind], kind, i)
+                    ag_unit(R["x"].at[kind], kind, i, u)
+
+        rs_drain(bank, i)
 
     def fin_copy(which, i):
         source = (R["r"], R["g"])[which]
@@ -818,19 +828,6 @@
         residual(1, i, pl.ds(G_DOWN + l, 1), None if last else 0)
         if last:
             fin_start(0, i)
-
-    def send_grad(slot, kind, i):
-        buf = R["e"].at[slot]
-
-        @when(inner)
-        def _():
-            def body(c):
-                here = at(i, c)
-                buf[here, half_cols] = R["g"][here].astype(BF16)
-
-            chunks(ROWS, body, True)
-
-        ag_start(buf, kind, i)
 
     def b2(l, i):
         e = R["e"].at[2 * l + 1]
@@ -848,7 +845,7 @@
             R["sv"][l, row] = R["sv"][l, row] + jnp.sum(dz, axis=0, keepdims=True)
             return 0
 
-        lax.fori_loop(0, hidden // width, body, 0)
+        lax.fori_loop(0, hidden // width, body, 0, unroll=True)
 
         def block(j):
             return dot_t(R["f"][rows(i)], R["wf"][l, block_rows(j), 0:hidden])
@@ -864,7 +861,6 @@
         R["do"][...] = dot(e[rows(i), :], R["wp"][l]).astype(BF16)
         if i == images - 1:
             grad_out(l)
-        factor = 1.0 / math.sqrt(HEAD_DIM)
         dos = [R["do"][:, lanes] for lanes in head_lanes]
         dps = [dot_t(dos[h], R["v"][l, keys, head_lanes[h]]) for h in range(heads)]
         dvs, dss = [], []
@@ -872,8 +868,8 @@
             prob = R["prob"][(l * images + i) * heads + h]
             dvs.append(t_dot(prob.astype(BF16), dos[h])[0:ROWS])
             delta = jnp.sum(prob * dps[h], axis=1, keepdims=True)
-            dss.append((prob * (dps[h] - delta) * factor).astype(BF16))
-        dqs = [dot(dss[h], R["k"][l, keys, head_lanes[h]]) for h in range(heads)]
+            dss.append((prob * (dps[h] - delta)).astype(BF16))
+        dqs = [dot(dss[h], R["k"][l, keys, head_lanes[h]]) * factor for h in range(heads)]
         dks = [t_dot(dss[h], R["q"][l, rows(i), head_lanes[h]])[0:ROWS] for h in range(heads)]
         dq, dk, dv = [jnp.concatenate(parts, axis=1) for parts in (dqs, dks, dvs)]
         for part, value in ((0, dq), (1, dk), (2, dv)):
@@ -895,31 +891,38 @@
     def add_down(l, i):
         @when(inner)
         def _():
-            def body(c, total):
-                return total + jnp.sum(R["g"][at(i, c * CHUNK)], axis=0, keepdims=True)
-
-            zero = jnp.zeros((1, 2 * width), F32)
-            half_add(l, V_DOWN, lax.fori_loop(0, ROWS // CHUNK, body, zero, unroll=True))
+            for u in range(2):
+                lanes = slice(u * width, (u + 1) * width)
+
+                def body(c, total):
+                    value = R["g"][at(i, c * CHUNK), lanes]
+                    return total + jnp.sum(value, axis=0, keepdims=True)
+
+                zero = jnp.zeros((1, width), F32)
+                total = lax.fori_loop(0, ROWS // CHUNK, body, zero, unroll=True)
+                small_add(l, u, V_DOWN, total)
 
     def post_b2(l, i):
         @when(l < LAYERS - 1)
         def _():
             ag_drain(R["e"].at[2 * l + 1], 2, i)
 
-        norm_back(0, l, 1, i, V_OUT)
-        send_grad(2 * l, 3, i)
+        norm_back(0, l, 1, i, R["e"].at[2 * l], 3)
+        norm_sums(0, l, 1, i, V_OUT)
 
     def post_b1(l, i):
         ag_drain(R["e"].at[2 * l], 3, i)
-        norm_back(1, l, 0, i, None)
 
         @when(l > 0)
         def _():
-            send_grad(2 * l - 1, 2, i)
+            norm_back(1, l, 0, i, R["e"].at[2 * l - 1], 2)
 
         @when(l == 0)
         def _():
+            norm_back(1, l, 0, i, None, None)
             fin_start(1, i)
+
+        norm_sums(1, l, 0, i, None)
 
     def grad_block(b):
         block = (mine * 2 * per_row // 256 + 1 + b) % (D // 256)
@@ -1023,13 +1026,15 @@
     for q in range(3):
         gn_copy(q, q, mate).wait_send()
     w_relay(0, 0)
-    for i in image:
+
+    def arrived(i):
         a0_finish(first_x, 0, i)
 
-    @when(inner)
-    def _():
-        R["r"][...] = first_x[:, half_cols].astype(F32)
-
+        @when(inner)
+        def _():
+            R["r"][rows(i)] = first_x[rows(i), half_cols].astype(F32)
+
+    arrived(0)
     w_finish(0, 0)
     for i in image:
         a0_relay(last_e, 1, i)
@@ -1042,6 +1047,12 @@
             ag_relay(R["x"].at[0], 0, 1)
 
         rs_relay(0, 0)
+
+        @when(l == 0)
+        def _():
+            for i in range(1, images):
+                arrived(i)
+
         f1(l, 1)
         post_f1(l, 0)
         w_relay(l, 2)

time: 237 us -> 228 us (0.962)
  Pallas kernels: 236 us -> 228 us
    pallas_call x1, Pallas kernels: 232 us -> 224 us  [body(): pl.pallas_call(functools.partial(kernel, wide, images, width, hidden, nam...]
where the time goes in v4:
time: 228 us
  Pallas kernels  228 us (100%)
    pallas_call x1, Pallas kernels, body(): pl.pallas_call(functools.partial(kernel, wide, images, width, hidden, nam...  224 us

profile of v4, /device:TPU:0, one launch (start us, length us, event | category | flops | bytes accessed | tf_op | source)
XLA Modules:
  0.0 228.3 jit_solution(3921191133838771256)
XLA Ops:
  0.6 223.7 %encoder_step.1 = (f32[394,256]{1,0:T(8,128)}, f32[394,256]{1,0:T(8,128)}, f32[2,2,256]{2,1,0:T(2,128)}, f32[2,2,256]{2,1,0:T(2,128)}, f32[2,3,128,256]{3,2,1,0:...) custom-call(bf16[394,256]{1,0:T(8,128)(2,1)} %refs_0_.1, ...), custom_call_target="tpu_custom_call" | custom-call | tf_op jit(solution)/shard_map/encoder_step/pallas_call | solution.py:1196
  224.3 3.8 %deliver.1 = (f32[394,256]{1,0:T(8,128)}, f32[394,256]{1,0:T(8,128)}, f32[2,2,256]{2,1,0:T(2,128)}, f32[2,2,256]{2,1,0:T(2,128)}, f32[2,3,128,256]{3,2,1,0:T(8,1...) custom-call(f32[394,256]{1,0:T(8,128)} %get-tuple-element.36.refs_0_, ...), custom_call_target="tpu_custom_call" | custom-call | tf_op jit(solution)/shard_map/deliver/pallas_call | solution.py:1227

commit v5 on v4

--- a/solution.py
+++ b/solution.py
@@ -606,8 +606,11 @@
         @when(inner)
         def _():
             t_total(i)
-            for u in range(2):
-                lanes = slice(u * width, (u + 1) * width)
+            for turn in range(2):
+                u = turn
+                if buf is None:
+                    u = 1 - inside if turn == 0 else inside
+                lanes = pl.ds(pl.multiple_of(u * width, 128), width)
                 scale = R["gn"][near_half + u, pl.ds(G_GAIN + at_norm, 1)]
                 rs_unit(bank, i, u)
 
@@ -629,6 +632,8 @@
                 chunks(ROWS, body, True)
                 if buf is not None:
                     ag_unit(buf, kind, i, u)
+                elif turn == 0:
+                    fin_copy(1, i).start()
 
     def norm_sums(bank, l, branch, i, out_row):
         rs_drain(bank, i)
@@ -920,7 +925,6 @@
         @when(l == 0)
         def _():
             norm_back(1, l, 0, i, None, None)
-            fin_start(1, i)
 
         norm_sums(1, l, 0, i, None)
 
@@ -1095,6 +1099,7 @@
 
         @when(top)
         def _():
+            post_f2(l, 0, True)
             rs_relay(1, 1)
 
         @when(l < LAYERS - 1)
@@ -1106,7 +1111,6 @@
 
         @when(top)
         def _():
-            post_f2(l, 0, True)
             post_f2(l, 1, True)
 
         grad_ffn(l, 0, 2)

time: 228 us -> 227 us (level)
  no operation moved by 1% of the time
where the time goes in v5:
time: 227 us
  Pallas kernels  226 us (100%)
    pallas_call x1, Pallas kernels, body(): pl.pallas_call(functools.partial(kernel, wide, images, width, hidden, nam...  222 us

profile of v5, /device:TPU:0, one launch (start us, length us, event | category | flops | bytes accessed | tf_op | source)
XLA Modules:
  0.0 226.7 jit_solution(2543681047334252980)
XLA Ops:
  0.6 222.0 %encoder_step.1 = (f32[394,256]{1,0:T(8,128)}, f32[394,256]{1,0:T(8,128)}, f32[2,2,256]{2,1,0:T(2,128)}, f32[2,2,256]{2,1,0:T(2,128)}, f32[2,3,128,256]{3,2,1,0:...) custom-call(bf16[394,256]{1,0:T(8,128)(2,1)} %refs_0_.1, ...), custom_call_target="tpu_custom_call" | custom-call | tf_op jit(solution)/shard_map/encoder_step/pallas_call | solution.py:1200
  222.7 3.8 %deliver.1 = (f32[394,256]{1,0:T(8,128)}, f32[394,256]{1,0:T(8,128)}, f32[2,2,256]{2,1,0:T(2,128)}, f32[2,2,256]{2,1,0:T(2,128)}, f32[2,3,128,256]{3,2,1,0:T(8,1...) custom-call(f32[394,256]{1,0:T(8,128)} %get-tuple-element.36.refs_0_, ...), custom_call_target="tpu_custom_call" | custom-call | tf_op jit(solution)/shard_map/deliver/pallas_call | solution.py:1231
